TPU v7x, 256 devices: a whole 4x4x8 slice. The times are simulated.
256 devices in a mesh: prow: 16 (over x, y), pcol: 16 (over z, core).
Axes of the slice: x: 4, y: 4, z: 8, core: 2. Of those that a mesh axis runs over, the one named last changes fastest.
Arguments:
- matrix: float32 [16384, 16384], P('prow', 'pcol'), may hold values from -6 to 6
- pivots: int32 [2, 512], replicated, may hold values from 512 to 16383, as said below
- lower_inverses: float32 [2, 512, 512], replicated, as said below
- upper_inverses: float32 [2, 512, 512], replicated, as said below
Outputs:
- factored: float32 [16384, 16384], P('prow', 'pcol')
Inputs may be any that keep to these rules, and one draw needn't show every extreme that they name: The 512 entries of pivots[j] are distinct and each is at least (j + 1) * 512. Each lower_inverses[j] is unit lower triangular. Each upper_inverses[j] is upper triangular with a positive diagonal.
All inputs are finite; a program needn't handle non-finite values.
Results may differ from a plain program's by a relative error of at most 0.0003.
Values sent between devices are 32-bit elements; how exact they have to be, the bound alone decides.
A program may use at most 128 MiB of HBM per device.

v0:
```python
import jax
import jax.numpy as jnp
from jax import lax
from jax.sharding import PartitionSpec as P


def spread(value, axis, source):
    kept = jnp.where(lax.axis_index(axis) == source, value, 0).astype(value.dtype)
    return lax.psum(kept, axis)


def body(matrix, pivots, lower_inverses, upper_inverses):
    row_count = lax.axis_size("prow")
    col_count = lax.axis_size("pcol")
    my_row = lax.axis_index("prow")
    my_col = lax.axis_index("pcol")
    rows_local, cols_local = matrix.shape
    panel_width = lower_inverses.shape[1]
    row_blocks = jnp.arange(rows_local, dtype=jnp.int32) // panel_width * row_count + my_row
    col_blocks = jnp.arange(cols_local, dtype=jnp.int32) // panel_width * col_count + my_col
    current = matrix
    for panel_step in range(pivots.shape[0]):
        targets = pivots[panel_step]
        global_blocks = targets // panel_width
        owner_row = global_blocks % row_count
        local_slot = global_blocks // row_count * panel_width + targets % panel_width
        is_mine = owner_row == my_row
        picked = jnp.where(is_mine[:, None], current[local_slot], 0.0)
        old_top = spread(current[:panel_width], "prow", panel_step)
        inverse_lower = lower_inverses[panel_step]
        new_top = lax.psum(picked, "prow")
        formed = jnp.dot(
            inverse_lower,
            new_top,
            precision=lax.Precision.HIGHEST,
            preferred_element_type=jnp.float32,
        )
        top_rows = jnp.where((col_blocks > panel_step)[None, :], formed, new_top)
        dropped_slot = jnp.where(is_mine, local_slot, rows_local)
        current = current.at[dropped_slot].set(old_top, mode="drop")
        on_diagonal = my_row == panel_step
        current = current.at[:panel_width].set(
            jnp.where(on_diagonal, top_rows, current[:panel_width])
        )
        column = spread(current[:, :panel_width], "pcol", panel_step)
        lower_full = jnp.dot(
            column,
            upper_inverses[panel_step],
            precision=lax.Precision.HIGHEST,
            preferred_element_type=jnp.float32,
        )
        is_below = (row_blocks > panel_step)[:, None]
        lower_part = jnp.where(is_below, lower_full, 0.0)
        upper_part = jnp.where((col_blocks > panel_step)[None, :], top_rows, 0.0)
        current = current - jnp.dot(
            lower_part,
            upper_part,
            precision=lax.Precision.HIGHEST,
            preferred_element_type=jnp.float32,
        )
        current = current.at[:, :panel_width].set(
            jnp.where(is_below & (my_col == panel_step), lower_full, current[:, :panel_width])
        )
    return current


def solution(mesh):
    placed = (P("prow", "pcol"), P(), P(), P())
    return jax.shard_map(
        body, mesh=mesh, in_specs=placed, out_specs=P("prow", "pcol"), check_vma=False
    )
```

profile of v0, /device:TPU:35, one launch (start us, length us, event | category | flops | bytes accessed | tf_op | source)
XLA Modules:
  0.0 602.2 jit_solution(10775062891973166959)
XLA Ops:
  6.5 0.0 copy-start.2
  6.5 0.0 all-reduce.13.cloned.1.call-start
  6.5 4.8 copy.55
  11.3 0.0 copy-done.2
  11.5 5.8 gather_fusion
  17.3 0.0 slice-start
  17.3 3.1 copy.21
  20.3 0.0 slice-done
  20.4 1.8 copy.41
  22.2 4.2 broadcast_select_fusion.1
  26.4 0.0 all-reduce.13.cloned.1.call-update
  26.4 0.0 all-reduce.7.cloned.1.call-start
  26.5 116.1 %all-reduce.13.cloned.1.call-done = (f32[512,1024]{0,1:T(8,128)}, f32[512,1024]{0,1:T(8,128)}) async-done(((f32[512,1024]{0,1:T(8,128)}, f32[512,1024]{0,1:T(8,128)}), (f32[512,1024]{0,1:T(8,128)}, f32[512,1024]{0,1:T(8,128)})) %all-reduce.13.cloned.1.call-update) | async-done | bytes 4194320 | tf_op jit(solution)/shard_map/psum | solution.py:9
  142.7 1.9 copy.20
  144.6 6.4 %scatter_fusion = f32[1024,1024]{1,0:T(8,128)} fusion(f32[1024,1024]{1,0:T(8,128)} %copy.55, s32[512]{0:T(512)S(1)} %bitcast.54, f32[512,1024]{1,0:T(8,128)S(1)} %copy.20), kind=kCustom, calls=%fused_computation.2 | custom fusion | bytes 6293504 | tf_op jit(solution)/shard_map/scatter | solution.py:40
  151.0 5.4 copy.23
  156.4 8.1 %fusion.3 = (f32[1024,1024]{0,1:T(8,128)}, f32[512,1024]{0,1:T(8,128)S(1)}) fusion(f32[1024,1024]{0,1:T(8,128)} %copy.23, pred[]{:T(512)S(6)} %eq.59, f32[512,1024]{0,1:T(8,128)} %get-tuple-element.56, f32[2,512,512]{2,1,0:T(8,128)} %param.14, pred[1024]{0:T(1024)(128)(4,1)S(1)} %fusion.32), kind=kOutput, calls=%fused_computation.16 | convolution fusion | flops 3222274048 | bytes 11535361 | tf_op jit(solution)/shard_map/dot_general | solution.py:32
  164.4 3.2 slice_select_fusion.3
  167.6 0.0 all-reduce.7.cloned.1.call-update
  167.6 0.2 all-reduce.11.cloned.1.call-start
  167.9 0.6 compare_reduce_fusion
  168.5 112.3 %all-reduce.7.cloned.1.call-done = f32[1024,512]{0,1:T(8,128)} async-done(((f32[1024,512]{0,1:T(8,128)}), f32[1024,512]{0,1:T(8,128)}) %all-reduce.7.cloned.1.call-update) | async-done | bytes 2097168 | tf_op jit(solution)/shard_map/psum | solution.py:9
  280.9 0.0 copy-start
  280.9 5.5 fusion.11
  286.4 0.0 copy-done
  286.4 8.7 %convolution_subtract_fusion.1 = f32[1024,1024]{0,1:T(8,128)} fusion(f32[1024,1024]{0,1:T(8,128)S(1)} %copy-done, f32[512,1024]{0,1:T(8,128)S(1)} %get-tuple-element.67, f32[1024,512]{0,1:T(8,128)S(1)} %fusion.11, pred[1024]{0:T(1024)(128)(4,1)S(1)} %fusion.32, pred[1024]{0:T(1024)(128)(4,1)S(1)} %get-tuple-element.70), kind=kOutput, calls=%fused_computation.7 | convolution fusion | flops 6444548096 | bytes 12584960 | tf_op jit(solution)/shard_map/dot_general | solution.py:55
  295.1 3.9 fusion
  299.0 5.4 copy.27
  304.4 3.2 slice_select_fusion.2
  307.6 5.0 gather_fusion.1
  312.6 1.8 copy.30
  314.4 3.1 broadcast_select_fusion
  317.6 0.0 all-reduce.11.cloned.1.call-update
  317.6 0.0 all-reduce.9.cloned.1.call-start
  317.7 116.3 %all-reduce.11.cloned.1.call-done = (f32[512,1024]{0,1:T(8,128)}, f32[512,1024]{0,1:T(8,128)}) async-done(((f32[512,1024]{0,1:T(8,128)}, f32[512,1024]{0,1:T(8,128)}), (f32[512,1024]{0,1:T(8,128)}, f32[512,1024]{0,1:T(8,128)})) %all-reduce.11.cloned.1.call-update) | async-done | bytes 4194320 | tf_op jit(solution)/shard_map/psum | solution.py:9
  434.0 1.9 copy.28
  435.9 6.3 %scatter_fusion.1 = f32[1024,1024]{1,0:T(8,128)} fusion(f32[1024,1024]{1,0:T(8,128)} %copy.27, s32[512]{0:T(512)S(1)} %bitcast.55, f32[512,1024]{1,0:T(8,128)S(1)} %copy.28), kind=kCustom, calls=%fused_computation.3 | custom fusion | bytes 6293504 | tf_op jit(solution)/shard_map/scatter | solution.py:40
  442.3 5.3 copy.32
  447.6 8.0 %fusion.2 = (f32[1024,1024]{0,1:T(8,128)}, f32[512,1024]{0,1:T(8,128)S(1)}) fusion(f32[1024,1024]{0,1:T(8,128)} %copy.32, pred[]{:T(512)S(6)} %eq.64, f32[512,1024]{0,1:T(8,128)} %get-tuple-element.54, f32[2,512,512]{2,1,0:T(8,128)} %param.14, pred[1024]{0:T(1024)(128)(4,1)S(1)} %fusion.31), kind=kOutput, calls=%fused_computation.12 | convolution fusion | flops 3222274048 | bytes 11535361 | tf_op jit(solution)/shard_map/dot_general | solution.py:32
  455.6 3.2 slice_select_fusion
  458.8 0.0 all-reduce.9.cloned.1.call-update
  458.9 113.2 %all-reduce.9.cloned.1.call-done = f32[1024,512]{0,1:T(8,128)} async-done(((f32[1024,512]{0,1:T(8,128)}), f32[1024,512]{0,1:T(8,128)}) %all-reduce.9.cloned.1.call-update) | async-done | bytes 2097168 | tf_op jit(solution)/shard_map/psum | solution.py:9
  572.1 0.0 copy-start.1
  572.1 5.5 fusion.8
  577.6 0.0 copy-done.1
  577.6 8.7 %convolution_subtract_fusion = f32[1024,1024]{0,1:T(8,128)} fusion(f32[1024,1024]{0,1:T(8,128)S(1)} %copy-done.1, f32[512,1024]{0,1:T(8,128)S(1)} %get-tuple-element.69, f32[1024,512]{0,1:T(8,128)S(1)} %fusion.8, pred[1024]{0:T(1024)(128)(4,1)S(1)} %fusion.31, pred[1024]{0:T(1024)(128)(4,1)S(1)} %fusion.33), kind=kOutput, calls=%fused_computation.6 | convolution fusion | flops 6444548096 | bytes 12584960 | tf_op jit(solution)/shard_map/dot_general | solution.py:55
  586.4 3.9 fusion.1
  590.3 5.3 copy.36
  (14 shorter events, 0.2 us)
Async XLA Ops:
  6.5 4.8 copy-start.2
  6.5 136.1 %all-reduce.13.cloned.1.call-start = ((), (), s32[]{:S(2)}) async-start(), calls=%async_computation.3 | async-start | bytes 8388608 | tf_op jit(solution)/shard_map/psum | solution.py:9
  17.3 3.1 slice-start
  26.4 254.4 %all-reduce.7.cloned.1.call-start = ((), (), s32[]{:S(2)}) async-start(), calls=%async_computation | async-start | bytes 4194304 | tf_op jit(solution)/shard_map/psum | solution.py:9
  167.6 266.4 %all-reduce.11.cloned.1.call-start = ((), (), s32[]{:S(2)}) async-start(), calls=%async_computation.2 | async-start | bytes 8388608 | tf_op jit(solution)/shard_map/psum | solution.py:9
  280.9 5.5 copy-start
  317.6 254.5 %all-reduce.9.cloned.1.call-start = ((), (), s32[]{:S(2)}) async-start(), calls=%async_computation.1 | async-start | bytes 4194304 | tf_op jit(solution)/shard_map/psum | solution.py:9
  572.1 5.5 copy-start.1
Sparse Core Ops, SparseCore 0:
  26.6 116.0 all-reduce.12
  167.8 113.0 all-reduce.6
  317.7 116.2 all-reduce.10
  459.0 113.0 all-reduce.8
where the time goes:
time: 606 us; the launch traced here: 602 us
  waiting for transfers between devices  458 us (76%)
  local copies, waits for them, and re-layouts  60.3 us (10%)
  matrix products  44.6 us (7%)
  other arithmetic  25.6 us (4%)
  between operations  13.3 us (2%)
    psum x4, waiting for transfers between devices, spread(): return lax.psum(kept, axis)  458 us
    scatter x4, local copies, waits for them, and re-layouts, body(): current = current.at[dropped_slot].set(old_top, mode='drop')  23.4 us
    dot_general x2, matrix products, body(): jnp.dot(lower_part, upper_part, precision=lax.Precision.HIGHEST, preferre...  17.5 us
    dot_general x2, matrix products, body(): jnp.dot(inverse_lower, new_top, precision=lax.Precision.HIGHEST, preferre...  16.1 us
    gather x4, local copies, waits for them, and re-layouts, body(): picked = jnp.where(is_mine[:, None], current[local_slot], 0.0)  15.7 us
  transfers between devices with their start and end apart: 4, of which 4 were waited for; matrix products, arithmetic and copies ran while one was open for 0% of the time, Pallas kernels for 0%

commit v1 on v0

v1 whole, which is shorter than its diff:
```python
import functools

import jax
import jax.numpy as jnp
from jax import lax
from jax.experimental import pallas as pl
from jax.experimental.pallas import tpu as pltpu
from jax.sharding import PartitionSpec as P

NB = 512
CAP = 96
CHUNK = 32
BLOCK = CAP + 2 * CHUNK
ZROWS = 32
SKEW = 2
VM = pltpu.VMEM
SM = pltpu.SMEM
F32 = jnp.float32
BF16 = jnp.bfloat16


def spec(space):
    return pl.BlockSpec(memory_space=space)


def remote(src, dst, send, recv, where):
    return pltpu.make_async_remote_copy(
        src_ref=src, dst_ref=dst, send_sem=send, recv_sem=recv,
        device_id=where, device_id_type=pl.DeviceIdType.MESH,
    )


def tables(pivots, me):
    p0, p1 = pivots[0], pivots[1]
    i = jnp.arange(NB, dtype=jnp.int32)
    r = jnp.arange(2 * NB, dtype=jnp.int32)

    def held(rows, default):
        hit = jnp.max(jnp.where(rows[:, None] == p0[None, :], i[None, :] + 1, 0), axis=1)
        return jnp.where(hit > 0, hit - 1, default)

    t = jnp.concatenate([p0, held(p1, p1)])
    owner = (t >> 9) & 15
    local = ((t >> 13) << 9) | (t & 511)
    earlier = (owner[None, :] == owner[:, None]) & (r[None, :] < r[:, None])
    rank = jnp.sum(earlier.astype(jnp.int32), axis=1)
    k = jnp.arange(CAP, dtype=jnp.int32)
    mine = (owner == me)[None, :] & (rank[None, :] == k[:, None])
    pack = jnp.sum(jnp.where(mine, local[None, :], 0), axis=1)
    take = owner * BLOCK + rank
    second = held(i + NB, i + NB)
    g = (((r >> 9) << 4) + me) * NB + (r & 511)
    m1 = jnp.max(jnp.where(g[:, None] == p1[None, :], second[None, :] + 1, 0), axis=1)
    m0 = jnp.max(jnp.where(g[:, None] == p0[None, :], i[None, :] + 1, 0), axis=1)
    src = jnp.where(g < 2 * NB, -1, jnp.where(m1 > 0, m1, m0) - 1)
    old = jnp.where(
        src >= 0,
        ((src & 511) >> 5) * BLOCK + CAP + (src >> 9) * CHUNK + (src & 31),
        -1,
    )
    return pack, take, old, jnp.max(rank) < CAP


def gather_kernel(pack_ref, a_ref, g_ref, sta, stb, sc_send, sca_recv, scb_recv,
                  sc2_send, sc2_recv, loc_sem, ag_send, ag_recv):
    p = lax.axis_index("prow")
    x, y = p // 4, p % 4

    def at(px, py):
        return {"prow": px * 4 + py}

    def copy_row(k, carry):
        l = pack_ref[k]
        g_ref[p, pl.ds(k, 1), :] = a_ref[l // 128, (l // 32) % 4, pl.ds(l % 32, 1), :]
        return carry

    barrier = pltpu.get_barrier_semaphore()
    for d in (1, 2, 3):
        pl.semaphore_signal(barrier, inc=1, device_id=at((x + d) % 4, y),
                            device_id_type=pl.DeviceIdType.MESH)
        pl.semaphore_signal(barrier, inc=1, device_id=at(x, (y + d) % 4),
                            device_id_type=pl.DeviceIdType.MESH)
    lax.fori_loop(0, CAP, copy_row, 0)
    pl.semaphore_wait(barrier, 6)

    halves = (pl.ds(0, 512), pl.ds(512, 512))

    def old(panel):
        return pl.ds(CAP + panel * CHUNK, CHUNK)

    def first_a(panel, d):
        c = (x + d) % 4
        return remote(a_ref.at[c, :, :, halves[0]], sta, sc_send.at[d - 1],
                      sca_recv.at[0], at(c, y))

    def first_b(panel, d):
        c = (y + d) % 4
        return remote(a_ref.at[pl.ds(0, 4), c, :, halves[1]], stb.at[panel],
                      sc_send.at[d + 2], scb_recv.at[panel], at(x, c))

    def second_a(panel, d, src):
        c = (y + d) % 4
        return remote(src.at[c], g_ref.at[p // 4 * 4 + c, old(panel), halves[0]],
                      sc2_send.at[panel * 6 + d - 1], sc2_recv.at[panel * 2],
                      at(x, c))

    def second_b(panel, d, src):
        c = (x + d) % 4
        return remote(src.at[c], g_ref.at[c * 4 + y, old(panel), halves[1]],
                      sc2_send.at[panel * 6 + d + 2], sc2_recv.at[panel * 2 + 1],
                      at(c, y))

    def own(panel, half, src):
        return pltpu.make_async_copy(src, g_ref.at[p, old(panel), halves[half]],
                                     loc_sem.at[panel * 2 + half])

    for panel in range(2):
        @pl.when(p == panel)
        def _():
            for d in (2, 1, 3):
                first_a(panel, d).start()
                first_b(panel, d).start()
            for d in (2, 1, 3):
                second_a(panel, d, a_ref.at[0, :, :, halves[0]]).start()
                second_b(panel, d, a_ref.at[pl.ds(0, 4), panel, :, halves[1]]).start()
            own(panel, 0, a_ref.at[0, panel, :, halves[0]]).start()
            own(panel, 1, a_ref.at[0, panel, :, halves[1]]).start()

    def coords(half, du, dv):
        if half == 0:
            return (x + du) % 4, (y + dv) % 4
        return (x + dv) % 4, (y + du) % 4

    def ag(part, lo, n):
        m = n // 2

        def piece(half, du, dv, r0, rows):
            bx, by = coords(half, du, dv)
            return g_ref.at[bx * 4 + by, pl.ds(lo + r0, rows), halves[half]]

        def cp(half, slot, du, dv, r0, rows, tu, tv):
            ref = piece(half, du, dv, r0, rows)
            s = (part * 2 + half) * 20 + slot
            return remote(ref, ref, ag_send.at[s], ag_recv.at[s], at(*coords(half, tu, tv)))

        def st1(half, which):
            return cp(half, which, *(
                (0, 0, 0, n, 1, 0),
                (0, 0, 0, n, 3, 0),
                (3, 0, 0, m, 1, 0),
                (1, 0, m, m, 3, 0),
            )[which])

        shift = (0, 3, 1, 2)

        def st2(half, j, which):
            u = shift[j]
            s = 4 + j * 4
            return cp(half, s + which, *(
                (u, 0, 0, n, 0, 1),
                (u, 0, 0, n, 0, 3),
                (u, 3, 0, m, 0, 1),
                (u, 1, m, m, 0, 3),
            )[which])

        hs = (0, 1)
        for h in hs:
            st1(h, 0).start()
            st1(h, 1).start()
        for h in hs:
            st2(h, 0, 0).start()
            st2(h, 0, 1).start()
        yield
        for h in hs:
            st1(h, 0).wait_recv()
            st1(h, 2).start()
            st1(h, 1).wait_recv()
            st1(h, 3).start()
        for h in hs:
            for j in (1, 2):
                st2(h, j, 0).start()
                st2(h, j, 1).start()
        for h in hs:
            st1(h, 2).wait_recv()
            st1(h, 3).wait_recv()
            st2(h, 3, 0).start()
            st2(h, 3, 1).start()
        yield
        for j in range(4):
            for h in hs:
                st2(h, j, 0).wait_recv()
                st2(h, j, 2).start()
                st2(h, j, 1).wait_recv()
                st2(h, j, 3).start()
        yield
        for j in range(4):
            for h in hs:
                st2(h, j, 2).wait_recv()
                st2(h, j, 3).wait_recv()
        for h in hs:
            for w in range(4):
                st1(h, w).wait_send()
                for j in range(4):
                    st2(h, j, w).wait_send()
        yield

    packed = ag(0, 0, CAP)
    next(packed)

    for panel in range(2):
        @pl.when((y == panel) & (x != 0))
        def _():
            first_a(panel, 1).wait_recv()
            for d in (2, 1, 3):
                second_a(panel, d, sta).start()
            own(panel, 0, sta.at[panel]).start()

        @pl.when((x == 0) & (y != panel))
        def _():
            first_b(panel, 1).wait_recv()
            for d in (2, 1, 3):
                second_b(panel, d, stb.at[panel]).start()
            own(panel, 1, stb.at[panel, 0]).start()

    next(packed)

    for panel in range(2):
        @pl.when(y == panel)
        def _():
            own(panel, 0, sta.at[panel]).wait()

        @pl.when(y != panel)
        def _():
            second_a(panel, 1, sta).wait_recv()

        @pl.when(x == 0)
        def _():
            own(panel, 1, stb.at[panel, 0]).wait()

        @pl.when(x != 0)
        def _():
            second_b(panel, 1, stb.at[panel]).wait_recv()

    oldrows = ag(1, CAP, 2 * CHUNK)
    next(oldrows)
    next(packed)
    next(oldrows)
    next(packed)
    next(oldrows)
    next(oldrows)

    for panel in range(2):
        @pl.when(p == panel)
        def _():
            for d in (1, 2, 3):
                first_a(panel, d).wait_send()
                first_b(panel, d).wait_send()

        @pl.when(y == panel)
        def _():
            for d in (1, 2, 3):
                second_a(panel, d, sta).wait_send()

        @pl.when(x == 0)
        def _():
            for d in (1, 2, 3):
                second_b(panel, d, stb.at[panel]).wait_send()


def gather_rows(pack, matrix):
    return pl.pallas_call(
        gather_kernel,
        out_shape=jax.ShapeDtypeStruct((16, BLOCK, 1024), F32),
        in_specs=[spec(SM), spec(VM)],
        out_specs=spec(VM),
        scratch_shapes=[
            VM((4, CHUNK, 512), F32),
            VM((2, 4, CHUNK, 512), F32),
            pltpu.SemaphoreType.DMA((6,)),
            pltpu.SemaphoreType.DMA((1,)),
            pltpu.SemaphoreType.DMA((2,)),
            pltpu.SemaphoreType.DMA((12,)),
            pltpu.SemaphoreType.DMA((4,)),
            pltpu.SemaphoreType.DMA((4,)),
            pltpu.SemaphoreType.DMA((80,)),
            pltpu.SemaphoreType.DMA((80,)),
        ],
        compiler_params=pltpu.CompilerParams(collective_id=0, has_side_effects=True),
        name="gather_rows",
    )(pack, matrix.reshape(8, 4, CHUNK, 1024))


def unpack_kernel(take_ref, old_ref, a_ref, g_ref, b_ref, t_ref, z_ref):
    c = lax.axis_index("pcol")

    def top(r, carry):
        t_ref[pl.ds(r, 1), :] = g_ref[pl.ds(take_ref[r], 1), :]
        return carry

    lax.fori_loop(0, 2 * NB, top, 0, unroll=8)
    b_ref[...] = a_ref[...]

    def swap(r, carry):
        s = old_ref[r]

        @pl.when(s >= 0)
        def _():
            b_ref[pl.ds(r, 1), :] = g_ref[pl.ds(s, 1), :]

        return carry

    lax.fori_loop(0, 2 * NB, swap, 0, unroll=8)

    @pl.when(c < 2)
    def _():
        z_ref[0:1024, :] = b_ref[:, 0:NB]

    @pl.when(c == 0)
    def _():
        z_ref[1024:1536, :] = t_ref[NB:, 0:NB]

    @pl.when(c == 1)
    def _():
        z_ref[1024:1536, :] = t_ref[0:NB, 0:NB]


def unpack(take, old, matrix, gathered):
    return pl.pallas_call(
        unpack_kernel,
        out_shape=(
            jax.ShapeDtypeStruct((1024, 1024), F32),
            jax.ShapeDtypeStruct((1024, 1024), F32),
            jax.ShapeDtypeStruct((1536, NB), F32),
        ),
        in_specs=[spec(SM), spec(SM), spec(VM), spec(VM)],
        out_specs=(spec(VM), spec(VM), spec(VM)),
        name="unpack",
    )(take, old, matrix, gathered.reshape(16 * BLOCK, 1024))


def cast_kernel(n, z_ref, o_ref, up_send, up_recv, dn_send, dn_recv, sib_send, sib_recv, loc):
    c = lax.axis_index("pcol")
    z, core = c // 2, c % 2

    def at(pz, pc):
        return {"pcol": pz * 2 + pc}

    barrier = pltpu.get_barrier_semaphore()
    for dev in (at((z + 1) % 8, core), at((z + 7) % 8, core), at(z, 1 - core)):
        pl.semaphore_signal(barrier, inc=1, device_id=dev, device_id_type=pl.DeviceIdType.MESH)
    pl.semaphore_wait(barrier, 3)

    def rows(k):
        return pl.ds(pl.multiple_of(k * ZROWS, ZROWS), ZROWS)

    def hop(src, k, up):
        if up:
            return remote(src.at[rows(k)], o_ref.at[core, rows(k)], up_send.at[k],
                          up_recv.at[k], at((z + 1) % 8, core))
        return remote(src.at[rows(n + k)], o_ref.at[core, rows(n + k)], dn_send.at[k],
                      dn_recv.at[k], at((z + 7) % 8, core))

    def sib(src, k):
        return remote(src.at[rows(k)], o_ref.at[core, rows(k)], sib_send.at[k],
                      sib_recv.at[k], at(z, 1 - core))

    mine = o_ref.at[core]

    @pl.when(z == 0)
    def _():
        def step(k, carry):
            hop(z_ref, k, True).start()
            hop(z_ref, k, False).start()
            return carry
        lax.fori_loop(0, n, step, 0)

        def side(k, carry):
            sib(z_ref, k).start()
            return carry
        lax.fori_loop(0, 2 * n, side, 0)
        keep = pltpu.make_async_copy(z_ref, mine, loc)
        keep.start()
        keep.wait()

        def done(k, carry):
            hop(z_ref, k, True).wait_send()
            hop(z_ref, k, False).wait_send()
            return carry
        lax.fori_loop(0, n, done, 0)

    @pl.when(z != 0)
    def _():
        def step(t, carry):
            k0 = t - SKEW * z
            k1 = t - SKEW * (8 - z)

            @pl.when((k0 >= 0) & (k0 < n))
            def _():
                hop(mine, k0, True).wait_recv()

                @pl.when(z < 7)
                def _():
                    hop(mine, k0, True).start()
                sib(mine, k0).start()

            @pl.when((k1 >= 0) & (k1 < n))
            def _():
                hop(mine, k1, False).wait_recv()

                @pl.when(z > 1)
                def _():
                    hop(mine, k1, False).start()
                sib(mine, n + k1).start()
            return carry
        lax.fori_loop(SKEW, n + 7 * SKEW, step, 0)

        @pl.when(z < 7)
        def _():
            def done(k, carry):
                hop(mine, k, True).wait_send()
                return carry
            lax.fori_loop(0, n, done, 0)

        @pl.when(z > 1)
        def _():
            def done(k, carry):
                hop(mine, k, False).wait_send()
                return carry
            lax.fori_loop(0, n, done, 0)

    other = o_ref.at[1 - core]

    def finish(k, carry):
        sib(mine, k).wait_send()
        remote(other.at[rows(k)], other.at[rows(k)], sib_send.at[k], sib_recv.at[k],
               at(z, 1 - core)).wait_recv()
        return carry
    lax.fori_loop(0, 2 * n, finish, 0)


def broadcast_z(panel):
    n = panel.shape[0] // (2 * ZROWS)
    dma = pltpu.SemaphoreType.DMA
    return pl.pallas_call(
        functools.partial(cast_kernel, n),
        out_shape=jax.ShapeDtypeStruct((2,) + panel.shape, F32),
        in_specs=[spec(VM)],
        out_specs=spec(VM),
        scratch_shapes=[dma((n,)), dma((n,)), dma((n,)), dma((n,)),
                        dma((2 * n,)), dma((2 * n,)), dma],
        compiler_params=pltpu.CompilerParams(collective_id=1, has_side_effects=True),
        name="broadcast_z",
    )(panel)


def split(v):
    hi = v.astype(BF16)
    return hi, (v - hi.astype(F32)).astype(BF16)


def dot3(a, b):
    f = functools.partial(jnp.dot, preferred_element_type=F32)
    return f(a[0], b[0]) + (f(a[0], b[1]) + f(a[1], b[0]))


def put(ref, rows, cols, v):
    hi, lo = split(v)
    ref[0, rows, cols] = hi
    ref[1, rows, cols] = lo


def get(ref, rows, cols):
    return ref[0, rows, cols], ref[1, rows, cols]


def update_kernel(b_ref, t_ref, pp_ref, li_ref, ui_ref, f_ref, u_s, l_s, uc_s, li_s, ui_s):
    p = lax.axis_index("prow")
    c = lax.axis_index("pcol")
    full = pl.ds(0, NB)

    def tile(i, size=256):
        return pl.ds(pl.multiple_of(i * size, size), size)

    for j in range(2):
        li_s[2 * j], li_s[2 * j + 1] = split(li_ref[j])
        ui_s[2 * j], ui_s[2 * j + 1] = split(ui_ref[j])

    def inv(ref, j, rows, cols):
        return ref[2 * j, rows, cols], ref[2 * j + 1, rows, cols]

    @pl.loop(0, 2)
    def _(i):
        put(uc_s, full, tile(i), dot3(inv(li_s, 0, full, full), split(pp_ref[1, 1024:1536, tile(i)])))

    @pl.loop(0, 6)
    def _(i):
        put(l_s, tile(i), full, dot3(split(pp_ref[0, tile(i), :]), inv(ui_s, 0, full, full)))

    @pl.loop(0, 4)
    def _(i):
        left = get(l_s, tile(i), full)
        rest = pp_ref[1, tile(i), :] - dot3(left, get(uc_s, full, full))
        put(l_s, tile(i), pl.ds(NB, NB), dot3(split(rest), inv(ui_s, 1, full, full)))

    @pl.loop(0, 4)
    def _(i):
        cols = tile(i)
        u0 = dot3(inv(li_s, 0, full, full), split(t_ref[0:NB, cols]))
        put(u_s, full, cols, u0)
        t1 = t_ref[NB:, cols] - dot3(get(l_s, pl.ds(1024, NB), full), get(u_s, full, cols))
        u1 = dot3(inv(li_s, 1, full, full), split(t1))
        put(u_s, pl.ds(NB, NB), cols, u1)

        @pl.loop(0, 4)
        def _(k):
            rows = tile(k)
            f_ref[rows, cols] = b_ref[rows, cols] - dot3(
                get(l_s, rows, pl.ds(0, 2 * NB)), get(u_s, pl.ds(0, 2 * NB), cols))

        @pl.when(p == 0)
        def _():
            f_ref[0:NB, cols] = u0

            @pl.when((c == 0) & (i < 2))
            def _():
                f_ref[0:NB, cols] = t_ref[0:NB, cols]

        @pl.when(p == 1)
        def _():
            f_ref[0:NB, cols] = u1

            @pl.when((c == 1) & (i < 2))
            def _():
                f_ref[0:NB, cols] = t1

    def lower(src, dst, part):
        f_ref[dst, 0:NB] = (l_s[0, src, part].astype(F32) + l_s[1, src, part].astype(F32))

    for j in range(2):
        part = pl.ds(j * NB, NB)

        @pl.when(c == j)
        def _():
            lower(pl.ds(NB, NB), pl.ds(NB, NB), part)

            @pl.when(p > j)
            def _():
                lower(full, full, part)

    @pl.when((c == 0) & (p == 1))
    def _():
        lower(pl.ds(1024, NB), full, full)


def update(b, t, pp, li, ui):
    return pl.pallas_call(
        update_kernel,
        out_shape=jax.ShapeDtypeStruct((1024, 1024), F32),
        in_specs=[spec(VM)] * 5,
        out_specs=spec(VM),
        scratch_shapes=[
            VM((2, 1024, 1024), BF16),
            VM((2, 1536, 1024), BF16),
            VM((2, NB, NB), BF16),
            VM((4, NB, NB), BF16),
            VM((4, NB, NB), BF16),
        ],
        name="update",
    )(b, t, pp, li, ui)


def spread(value, axis, source):
    kept = jnp.where(lax.axis_index(axis) == source, value, 0).astype(value.dtype)
    return lax.psum(kept, axis)


def general(matrix, pivots, lower_inverses, upper_inverses):
    my_row = lax.axis_index("prow")
    my_col = lax.axis_index("pcol")
    rows_local, cols_local = matrix.shape
    dot = functools.partial(jnp.dot, precision=lax.Precision.HIGH, preferred_element_type=F32)
    row_blocks = jnp.arange(rows_local, dtype=jnp.int32) // NB * 16 + my_row
    col_blocks = jnp.arange(cols_local, dtype=jnp.int32) // NB * 16 + my_col

    def panel(step, current):
        targets = pivots[step]
        blocks = targets // NB
        slot = blocks // 16 * NB + targets % NB
        is_mine = blocks % 16 == my_row
        picked = jnp.where(is_mine[:, None], current[slot], 0.0)
        old_top = spread(current[:NB], "prow", step)
        new_top = lax.psum(picked, "prow")
        after = (col_blocks > step)[None, :]
        top = jnp.where(after, dot(lower_inverses[step], new_top), new_top)
        current = current.at[jnp.where(is_mine, slot, rows_local)].set(old_top, mode="drop")
        current = current.at[:NB].set(jnp.where(my_row == step, top, current[:NB]))
        column = spread(current[:, :NB], "pcol", step)
        below = (row_blocks > step)[:, None]
        lower = jnp.where(below, dot(column, upper_inverses[step]), 0.0)
        current = current - dot(lower, jnp.where(after, top, 0.0))
        return current.at[:, :NB].set(
            jnp.where(below & (my_col == step), lower, current[:, :NB]))

    return lax.fori_loop(0, 2, panel, matrix)


def fast(matrix, pack, take, old, li, ui):
    gathered = gather_rows(pack, matrix)
    b, t, z = unpack(take, old, matrix, gathered)
    return update(b, t, broadcast_z(z), li, ui)


def body(matrix, pivots, lower_inverses, upper_inverses):
    pack, take, old, fits = tables(pivots, lax.axis_index("prow"))
    return lax.cond(
        fits,
        lambda: fast(matrix, pack, take, old, lower_inverses, upper_inverses),
        lambda: general(matrix, pivots, lower_inverses, upper_inverses),
    )


def solution(mesh):
    placed = (P("prow", "pcol"), P(), P(), P())
    return jax.shard_map(
        body, mesh=mesh, in_specs=placed, out_specs=P("prow", "pcol"), check_vma=False
    )
```

time: 606 us -> 243 us (0.40)
  waiting for transfers between devices: 458 us -> 0 us
  Pallas kernels: 0 us -> 219 us
  local copies, waits for them, and re-layouts: 60.3 us -> 4.86 us
  matrix products: 44.6 us -> 0 us
  other arithmetic: 25.6 us -> 3.77 us
    psum x4 -> x0, waiting for transfers between devices: 458 us -> none  [spread(): return lax.psum(kept, axis)]
    pallas_call x0 -> x4, Pallas kernels: none -> 219 us  [the longest x1 80.9 us: gather_rows(): pl.pallas_call(gather_kernel, out_shape=jax.ShapeDtypeStruct((16, BLOCK,...]
    dot_general x6 -> x0, matrix products: 44.6 us -> none  [the longest x2 17.5 us: body(): jnp.dot(lower_part, upper_part, precision=lax.Precision.HIGHEST, preferre...]
    scatter x6 -> x0, local copies, waits for them, and re-layouts: 34.1 us -> none  [the longest x4 23.4 us: body(): current = current.at[dropped_slot].set(old_top, mode='drop')]
    select_n x9 -> x3, other arithmetic: 17 us -> 0.03 us  [the longest x2 0.02 us: held(): return jnp.where(hit > 0, hit - 1, default)]
    gather x4 -> x0, local copies, waits for them, and re-layouts: 15.7 us -> none  [body(): picked = jnp.where(is_mine[:, None], current[local_slot], 0.0)]
    scatter x2 -> x0, other arithmetic: 7.84 us -> none  [body(): current.at[:, :panel_width]]
  transfers between devices with their start and end apart: 4 -> 0, of which waited for: 4 -> 0; matrix products, arithmetic and copies ran while one was open for 0% -> 0% of each run, Pallas kernels for 0% -> 0%
where the time goes in v1:
time: 243 us; the launch traced here: 242 us
  Pallas kernels  219 us (90%)
  between operations  14.2 us (6%)
  local copies, waits for them, and re-layouts  4.86 us (2%)
  other arithmetic  3.77 us (2%)
    pallas_call x1, Pallas kernels, gather_rows(): pl.pallas_call(gather_kernel, out_shape=jax.ShapeDtypeStruct((16, BLOCK,...  80.9 us
    pallas_call x1, Pallas kernels, broadcast_z(): pl.pallas_call(functools.partial(cast_kernel, n), out_shape=jax.ShapeDtyp...  78.8 us
    pallas_call x1, Pallas kernels, update(): pl.pallas_call(update_kernel, out_shape=jax.ShapeDtypeStruct((1024, 1024)...  36.2 us
    pallas_call x1, Pallas kernels, unpack(): pl.pallas_call(unpack_kernel, out_shape=(jax.ShapeDtypeStruct((1024, 1024...  23.6 us

profile of v1, /device:TPU:35, one launch (start us, length us, event | category | flops | bytes accessed | tf_op | source)
XLA Modules:
  0.0 242.4 jit_solution(6673355348175497258)
XLA Ops:
  6.5 0.0 copy-start.3
  6.5 4.8 %copy.24 = f32[1024,1024]{1,0:T(8,128)} copy(f32[1024,1024]{1,0:T(8,128)} %param.12) | data formatting | bytes 8388608
  11.4 0.0 copy-done.3
  11.4 0.4 select_reduce_fusion.3
  11.8 0.7 select_reduce_fusion.1
  12.6 0.5 convert_reduce_fusion
  13.1 0.7 reduce_max.46
  14.6 221.0 %conditional.1 = (f32[1024,1024]{1,0:T(8,128)}) conditional(s32[]{:T(128)} %convert_element_type.17, (s32[2,512]{1,0:T(2,128)S(1)}, f32[2,512,512]{2,1,0:T(8,128)}, f32[2,512,512]{2,1,0:T(8,128)}, f32[1024,1024]{1,0:T(8,128)}) %tuple.122, (f32[1024,1024]{1,0:T(8,128)}, s32[1024]{0:T(1024)S(1)}, s32[1024]{0:T(1024)S(1)}, s32[1024]{0:T(1024)S(1)}, ...), branch_computations={%region_7.15_spmd, %region_15.16_spmd} | conditional | flops 6450381824 | bytes 130061832 | solution.py:615
  14.8 0.6 fusion.9
  15.4 0.7 select_reduce_fusion.pack_ref
  16.2 80.9 %gather_rows.1 = f32[16,160,1024]{2,1,0:T(8,128)} custom-call(s32[96]{0:T(128)} %select_reduce_fusion.pack_ref, f32[8,4,32,1024]{3,2,1,0:T(8,128)} %bitcast.51), custom_call_target="tpu_custom_call" | custom-call | tf_op jit(solution)/shard_map/cond/branch_1_fun/gather_rows/pallas_call | solution.py:271
  97.1 23.6 %unpack.1 = (f32[1024,1024]{1,0:T(8,128)}, f32[1024,1024]{1,0:T(8,128)}, f32[1536,512]{1,0:T(8,128)}) custom-call(s32[1024]{0:T(1024)} %get-tuple-element.487.take_ref, s32[1024]{0:T(1024)} %get-tuple-element.486.old_ref, f32[1024,1024]{1,0:T(8,128)} %get-tuple-element.352.a_ref, f32[2560,1024]{1,0:T(8,128)} %bitcast.52), custom_call_target="tpu_custom_call" | custom-call | tf_op jit(solution)/shard_map/cond/branch_1_fun/unpack/pallas_call | solution.py:328
  120.6 0.0 copy-start.2
  120.6 78.8 %broadcast_z.1.pp_ref = f32[2,1536,512]{2,1,0:T(8,128)} custom-call(f32[1536,512]{1,0:T(8,128)} %get-tuple-element.356.z_ref), custom_call_target="tpu_custom_call" | custom-call | tf_op jit(solution)/shard_map/cond/branch_1_fun/broadcast_z/pallas_call | solution.py:444
  199.4 0.0 copy-done.2
  199.4 36.2 %update.1 = f32[1024,1024]{1,0:T(8,128)} custom-call(f32[1024,1024]{1,0:T(8,128)} %get-tuple-element.354.b_ref, f32[1024,1024]{1,0:T(8,128)} %get-tuple-element.355.t_ref, f32[2,1536,512]{2,1,0:T(8,128)} %broadcast_z.1.pp_ref, f32[2,512,512]{2,1,0:T(8,128)S(1)} %copy-done.2, f32[2,512,512]{2,1,0:T(8,128)} %get-tuple-element.358.ui_ref), custom_call_target="tpu_custom_call" | custom-call | tf_op jit(solution)/shard_map/cond/branch_1_fun/update/pallas_call | solution.py:556
  (16 shorter events, 0.1 us)
Async XLA Ops:
  6.5 4.8 %copy-start.3 = (s32[2,512]{1,0:T(2,128)S(1)}, s32[2,512]{1,0:T(2,128)}, u32[]{:S(2)}) copy-start(s32[2,512]{1,0:T(2,128)} %param.13) | copy-start | bytes 12292
  120.6 78.8 %copy-start.2 = (f32[2,512,512]{2,1,0:T(8,128)S(1)}, f32[2,512,512]{2,1,0:T(8,128)}, u32[]{:S(2)}) copy-start(f32[2,512,512]{2,1,0:T(8,128)} %get-tuple-element.357.li_ref) | copy-start | bytes 6291460 | tf_op jit(solution)/shard_map/cond

commit v2 on v0

v2 whole, which is shorter than its diff:
```python
import functools

import jax
import jax.numpy as jnp
from jax import lax
from jax.experimental import pallas as pl
from jax.experimental.pallas import tpu as pltpu
from jax.sharding import PartitionSpec as P

NB = 512
CAP = 96
CHUNK = 32
HALF = CAP // 2
ZROWS = 16
ROWS = 768 + HALF
STREAM = ROWS // ZROWS
SKEW = 5
VM = pltpu.VMEM
SM = pltpu.SMEM
F32 = jnp.float32
BF16 = jnp.bfloat16


def spec(space):
    return pl.BlockSpec(memory_space=space)


def remote(src, dst, send, recv, where):
    return pltpu.make_async_remote_copy(
        src_ref=src, dst_ref=dst, send_sem=send, recv_sem=recv,
        device_id=where, device_id_type=pl.DeviceIdType.MESH,
    )


def tables(pivots, me):
    p0, p1 = pivots[0], pivots[1]
    i = jnp.arange(NB, dtype=jnp.int32)
    r = jnp.arange(2 * NB, dtype=jnp.int32)

    def held(rows, default):
        hit = jnp.max(jnp.where(rows[:, None] == p0[None, :], i[None, :] + 1, 0), axis=1)
        return jnp.where(hit > 0, hit - 1, default)

    t = jnp.concatenate([p0, held(p1, p1)])
    owner = (t >> 9) & 15
    local = ((t >> 13) << 9) | (t & 511)
    earlier = (owner[None, :] == owner[:, None]) & (r[None, :] < r[:, None])
    rank = jnp.sum(earlier.astype(jnp.int32), axis=1)
    k = jnp.arange(CAP, dtype=jnp.int32)
    mine = (owner == me)[None, :] & (rank[None, :] == k[:, None])
    pack = jnp.sum(jnp.where(mine, local[None, :], 0), axis=1)
    take = owner * 256 + rank
    second = held(i + NB, i + NB)
    g = (((r >> 9) << 4) + me) * NB + (r & 511)
    m1 = jnp.max(jnp.where(g[:, None] == p1[None, :], second[None, :] + 1, 0), axis=1)
    m0 = jnp.max(jnp.where(g[:, None] == p0[None, :], i[None, :] + 1, 0), axis=1)
    src = jnp.where(g < 2 * NB, -1, jnp.where(m1 > 0, m1, m0) - 1)
    valid = src >= 0
    count = jnp.sum((valid[None, :] & (r[None, :] < r[:, None])).astype(jnp.int32), axis=1)
    chosen = valid[None, :] & (count[None, :] == k[:, None])
    cpos = jnp.sum(jnp.where(chosen, r[None, :], 0), axis=1)
    csrc = ((src & 511) >> 5) * 256 + (src >> 9) * CHUNK + (src & 31)
    csrc = jnp.sum(jnp.where(chosen, csrc[None, :], 0), axis=1)
    total = jnp.sum(valid.astype(jnp.int32)).reshape(1)
    return pack, take, csrc, cpos, total, jnp.max(rank) < CAP


def split(v):
    hi = v.astype(BF16)
    return hi, (v - hi.astype(F32)).astype(BF16)


def dot3(a, b):
    f = functools.partial(jnp.dot, preferred_element_type=F32)
    return f(a[0], b[0]) + (f(a[0], b[1]) + f(a[1], b[0]))


def put(ref, rows, cols, v):
    hi, lo = split(v)
    ref[0, rows, cols] = hi
    ref[1, rows, cols] = lo


def get(ref, rows, cols):
    return ref[0, rows, cols], ref[1, rows, cols]


def factor_kernel(pack_ref, take_ref, csrc_ref, a_ref, li_ref, ui_ref, f_ref, fc_ref,
                  sa_ref, oa_ref, sb_ref, ob_ref, pp_ref, t_ref, u_s, l_s, uc_s, li_s, ui_s, sta, stb,
                  sc_send, sca_recv, scb_recv, sc2_send, sc2_recv, loc_sem,
                  ag_send, ag_recv,
                  up_send, up_recv, dn_send, dn_recv, sib_send, sib_recv):
    p = lax.axis_index("prow")
    x, y = p // 4, p % 4
    c = lax.axis_index("pcol")
    z, core = c // 2, c % 2

    def at(px, py):
        return {"prow": px * 4 + py}

    def zat(pz, pc):
        return {"pcol": pz * 2 + pc}

    def signal(sem, where):
        pl.semaphore_signal(sem, inc=1, device_id=where,
                            device_id_type=pl.DeviceIdType.MESH)

    barrier = pltpu.get_barrier_semaphore()
    for d in (1, 2, 3):
        signal(barrier, at((x + d) % 4, y))
        signal(barrier, at(x, (y + d) % 4))
    signal(barrier, zat((z + 1) % 8, core))
    signal(barrier, zat((z + 7) % 8, core))
    signal(barrier, zat(z, 1 - core))

    def packed_row(k, carry):
        l = pack_ref[k]
        row = a_ref[l // 128, (l // 32) % 4, pl.ds(l % 32, 1), :]
        sa_ref[p, pl.ds(k, 1), :] = row[:, 0:NB]
        sb_ref[p, pl.ds(k, 1), :] = row[:, NB:]
        return carry

    lax.fori_loop(0, CAP, packed_row, 0, unroll=4)

    @pl.when(z == 0)
    def _():
        @pl.loop(0, 32)
        def _(i):
            pp_ref[core, i // 16, pl.ds(pl.multiple_of(i % 16 * 32, 32), 32), :] = (
                a_ref[i // 4, i % 4, :, 0:NB])

    for j in range(2):
        li_s[2 * j], li_s[2 * j + 1] = split(li_ref[j])
        ui_s[2 * j], ui_s[2 * j + 1] = split(ui_ref[j])

    pl.semaphore_wait(barrier, 9)

    def quarter(i):
        return pl.ds(256 * i, 256)

    packed, olds = (sa_ref, sb_ref), (oa_ref, ob_ref)

    def old(panel):
        return pl.ds(panel * CHUNK, CHUNK)

    def first_a(ab, panel, d):
        k = (x + d) % 4
        return remote(a_ref.at[k, :, :, quarter(2 * ab)], sta.at[ab],
                      sc_send.at[ab * 6 + d - 1], sca_recv.at[ab], at(k, y))

    def first_b(ab, panel, d):
        k = (y + d) % 4
        return remote(a_ref.at[pl.ds(0, 4), k, :, quarter(2 * ab + 1)], stb.at[ab, panel],
                      sc_send.at[ab * 6 + d + 2], scb_recv.at[ab * 2 + panel], at(x, k))

    def second_a(ab, panel, d, src):
        k = (y + d) % 4
        return remote(src.at[k], olds[ab].at[x * 4 + k, old(panel), quarter(0)],
                      sc2_send.at[ab * 12 + panel * 6 + d - 1],
                      sc2_recv.at[ab * 4 + panel * 2], at(x, k))

    def second_b(ab, panel, d, src):
        k = (x + d) % 4
        return remote(src.at[k], olds[ab].at[k * 4 + y, old(panel), quarter(1)],
                      sc2_send.at[ab * 12 + panel * 6 + d + 2],
                      sc2_recv.at[ab * 4 + panel * 2 + 1], at(k, y))

    def own(ab, panel, half, src):
        return pltpu.make_async_copy(src, olds[ab].at[p, old(panel), quarter(half)],
                                     loc_sem.at[ab * 4 + panel * 2 + half])

    def scatter(ab):
        qa, qb = quarter(2 * ab), quarter(2 * ab + 1)
        for panel in range(2):
            @pl.when(p == panel)
            def _():
                for d in (2, 1, 3):
                    first_a(ab, panel, d).start()
                    first_b(ab, panel, d).start()
                for d in (2, 1, 3):
                    second_a(ab, panel, d, a_ref.at[0, :, :, qa]).start()
                    second_b(ab, panel, d, a_ref.at[pl.ds(0, 4), panel, :, qb]).start()
                own(ab, panel, 0, a_ref.at[0, panel, :, qa]).start()
                own(ab, panel, 1, a_ref.at[0, panel, :, qb]).start()

    def relay(ab):
        for panel in range(2):
            @pl.when((y == panel) & (x != 0))
            def _():
                first_a(ab, panel, 1).wait_recv()
                for d in (2, 1, 3):
                    second_a(ab, panel, d, sta.at[ab]).start()
                own(ab, panel, 0, sta.at[ab, panel]).start()

            @pl.when((x == 0) & (y != panel))
            def _():
                first_b(ab, panel, 1).wait_recv()
                for d in (2, 1, 3):
                    second_b(ab, panel, d, stb.at[ab, panel]).start()
                own(ab, panel, 1, stb.at[ab, panel, 0]).start()

    def scattered(ab):
        for panel in range(2):
            @pl.when(y == panel)
            def _():
                own(ab, panel, 0, sta.at[ab, panel]).wait()

            @pl.when(y != panel)
            def _():
                second_a(ab, panel, 1, sta.at[ab]).wait_recv()

            @pl.when(x == 0)
            def _():
                own(ab, panel, 1, stb.at[ab, panel, 0]).wait()

            @pl.when(x != 0)
            def _():
                second_b(ab, panel, 1, stb.at[ab, panel]).wait_recv()

    def scatter_drain(ab):
        for panel in range(2):
            @pl.when(p == panel)
            def _():
                for d in (1, 2, 3):
                    first_a(ab, panel, d).wait_send()
                    first_b(ab, panel, d).wait_send()

            @pl.when(y == panel)
            def _():
                for d in (1, 2, 3):
                    second_a(ab, panel, d, sta.at[ab]).wait_send()

            @pl.when(x == 0)
            def _():
                for d in (1, 2, 3):
                    second_b(ab, panel, d, stb.at[ab, panel]).wait_send()

    def coords(half, du, dv):
        if half == 0:
            return (x + du) % 4, (y + dv) % 4
        return (x + dv) % 4, (y + du) % 4

    shift = (0, 3, 1, 2)
    hs = (0, 1)

    def all_gather(ab, kind):
        n = (CAP, 2 * CHUNK)[kind]
        buffer = (packed, olds)[kind][ab]
        m = n // 2
        part = ab * 2 + kind

        def cp(half, slot, du, dv, r0, rows, tu, tv):
            bx, by = coords(half, du, dv)
            ref = buffer.at[bx * 4 + by, pl.ds(r0, rows), quarter(half)]
            s = (part * 2 + half) * 20 + slot
            return remote(ref, ref, ag_send.at[s], ag_recv.at[s], at(*coords(half, tu, tv)))

        def st1(half, which):
            return cp(half, which, *(
                (0, 0, 0, n, 1, 0),
                (0, 0, 0, n, 3, 0),
                (3, 0, 0, m, 1, 0),
                (1, 0, m, m, 3, 0),
            )[which])

        def st2(half, j, which):
            u = shift[j]
            return cp(half, 4 + j * 4 + which, *(
                (u, 0, 0, n, 0, 1),
                (u, 0, 0, n, 0, 3),
                (u, 3, 0, m, 0, 1),
                (u, 1, m, m, 0, 3),
            )[which])

        for h in hs:
            st1(h, 0).start()
            st1(h, 1).start()
        for h in hs:
            st2(h, 0, 0).start()
            st2(h, 0, 1).start()
        yield
        for h in hs:
            st1(h, 0).wait_recv()
            st1(h, 2).start()
            st1(h, 1).wait_recv()
            st1(h, 3).start()
        for h in hs:
            for j in (1, 2):
                st2(h, j, 0).start()
                st2(h, j, 1).start()
        yield
        for h in hs:
            st1(h, 2).wait_recv()
            st1(h, 3).wait_recv()
            st2(h, 3, 0).start()
            st2(h, 3, 1).start()
        yield
        for j in range(4):
            for h in hs:
                st2(h, j, 0).wait_recv()
                st2(h, j, 2).start()
                st2(h, j, 1).wait_recv()
                st2(h, j, 3).start()
        yield
        for j in range(4):
            for h in hs:
                st2(h, j, 2).wait_recv()
                st2(h, j, 3).wait_recv()
        yield
        for h in hs:
            for w in range(4):
                st1(h, w).wait_send()
                for j in range(4):
                    st2(h, j, w).wait_send()
        yield

    def rows(k):
        return pl.ds(pl.multiple_of(k * ZROWS, ZROWS), ZROWS)

    def hop(k, d):
        ref = pp_ref.at[core, d, rows(k)]
        if d == 0:
            return remote(ref, ref, up_send.at[k], up_recv.at[k], zat((z + 1) % 8, core))
        return remote(ref, ref, dn_send.at[k], dn_recv.at[k], zat((z + 7) % 8, core))

    def sib(k, d, which):
        ref = pp_ref.at[which, d, rows(k)]
        s = d * STREAM + k
        return remote(ref, ref, sib_send.at[s], sib_recv.at[s], zat(z, 1 - core))

    def z_source(k0, k1):
        def step(k, carry):
            for d in (0, 1):
                hop(k, d).start()
            for d in (0, 1):
                sib(k, d, core).start()
            return carry
        lax.fori_loop(k0, k1, step, 0)

    def z_relay(t0, t1):
        @pl.when(z != 0)
        def _():
            def step(t, carry):
                for d in (0, 1):
                    k = t - SKEW * (z if d == 0 else 8 - z)

                    @pl.when((k >= 0) & (k < STREAM))
                    def _():
                        hop(k, d).wait_recv()

                        @pl.when(z != (7 if d == 0 else 1))
                        def _():
                            hop(k, d).start()
                        sib(k, d, core).start()
                return carry
            lax.fori_loop(t0, t1, step, 0)

    def z_finish():
        def got(k, carry):
            for d in (0, 1):
                sib(k, d, 1 - core).wait_recv()
            return carry
        lax.fori_loop(0, STREAM, got, 0)

    def z_drain():
        def sent(k, carry):
            for d in (0, 1):
                sib(k, d, core).wait_send()

                @pl.when(z != (7 if d == 0 else 1))
                def _():
                    hop(k, d).wait_send()
            return carry
        lax.fori_loop(0, STREAM, sent, 0)

    def landed(buffer, v):
        return buffer[v // 256, pl.ds(v % 256, 1), :]

    left, right = pl.ds(0, NB), pl.ds(NB, NB)

    def panel_tops():
        @pl.when(z == 0)
        def _():
            def one(r, carry):
                v = take_ref[r + NB * (1 - core)]
                pp_ref[core, r // 256, pl.ds(NB + r % 256, 1), :] = landed(sa_ref, v)
                return carry
            lax.fori_loop(0, NB, one, 0, unroll=8)
            z_source(32, 48)

    def panel_swapped():
        @pl.when(z == 0)
        def _():
            def one(k, carry):
                pp_ref[core, k // HALF, pl.ds(768 + k % HALF, 1), :] = landed(oa_ref, csrc_ref[k])
                return carry
            lax.fori_loop(0, CAP, one, 0, unroll=8)
            z_source(48, STREAM)

    sa, oa = all_gather(0, 0), all_gather(0, 1)
    sb, ob = all_gather(1, 0), all_gather(1, 1)
    next(sa)
    scatter(0)
    scatter(1)

    @pl.when(z == 0)
    def _():
        z_source(0, 32)

    z_relay(5, 8)
    next(sa)
    z_relay(8, 13)
    next(sa)
    relay(0)
    z_relay(13, 20)
    relay(1)
    next(sb)
    z_relay(20, 26)
    next(sa)
    scattered(0)
    next(oa)
    z_relay(26, 32)
    next(oa)
    z_relay(32, 36)
    next(oa)
    next(sa)
    panel_tops()
    z_relay(36, 44)
    next(oa)
    next(sb)
    z_relay(44, 50)
    next(oa)
    panel_swapped()
    next(sb)
    scattered(1)
    next(ob)
    z_relay(50, 60)
    next(sb)
    next(ob)
    z_relay(60, 68)
    next(ob)
    next(sb)
    z_relay(68, STREAM + 7 * SKEW)
    next(ob)
    z_finish()

    full = pl.ds(0, NB)

    def tile(i, size=256):
        return pl.ds(pl.multiple_of(i * size, size), size)

    def lrow(d, r, n):
        return pl.ds(pl.multiple_of(d * ROWS + r, 16), n)

    def inv(ref, j, r, k):
        return ref[2 * j, r, k], ref[2 * j + 1, r, k]

    def top_row(r, carry):
        v = take_ref[r]
        t_ref[pl.ds(r, 1), left] = landed(sa_ref, v)
        t_ref[pl.ds(r, 1), right] = landed(sb_ref, v)
        return carry

    lax.fori_loop(0, 2 * NB, top_row, 0, unroll=8)

    def lower0(d, r, n):
        src = pl.ds(pl.multiple_of(r, 16), n)
        put(l_s, lrow(d, r, n), full, dot3(split(pp_ref[0, d, src, :]), inv(ui_s, 0, full, full)))

    def lower1(d, r, n):
        src = pl.ds(pl.multiple_of(r, 16), n)
        rest = pp_ref[1, d, src, :] - dot3(get(l_s, lrow(d, r, n), full), get(uc_s, full, full))
        put(l_s, lrow(d, r, n), pl.ds(NB, NB), dot3(split(rest), inv(ui_s, 1, full, full)))

    @pl.loop(0, 2)
    def _(i):
        uc = sum(
            dot3(inv(li_s, 0, full, tile(d)), split(pp_ref[1, d, pl.ds(NB, 256), tile(i)]))
            for d in (0, 1)
        )
        put(uc_s, full, tile(i), uc)

    @pl.loop(0, 6)
    def _(i):
        lower0(i // 3, i % 3 * 256, 256)

    @pl.loop(0, 4)
    def _(i):
        lower1(i // 2, i % 2 * 256, 256)

    @pl.loop(0, 2)
    def _(d):
        lower0(d, 768, HALF)
        lower1(d, 768, HALF)

    next(ob)

    def swapped_row(k, carry):
        v = csrc_ref[k]
        fc_ref[pl.ds(k, 1), left] = landed(oa_ref, v)
        fc_ref[pl.ds(k, 1), right] = landed(ob_ref, v)
        return carry

    lax.fori_loop(0, CAP, swapped_row, 0, unroll=8)
    both = pl.ds(0, 2 * NB)

    @pl.loop(0, 4)
    def _(i):
        cols = tile(i)
        u0 = dot3(inv(li_s, 0, full, full), split(t_ref[0:NB, cols]))
        put(u_s, full, cols, u0)
        for d in (0, 1):
            rows2 = pl.ds(NB + 256 * d, 256)
            t_ref[rows2, cols] = t_ref[rows2, cols] - dot3(
                get(l_s, lrow(d, NB, 256), full), get(u_s, full, cols))
        t1 = t_ref[NB:, cols]
        u1 = dot3(inv(li_s, 1, full, full), split(t1))
        put(u_s, pl.ds(NB, NB), cols, u1)

        @pl.loop(0, 4)
        def _(k):
            r = tile(k)
            f_ref[r, cols] = a_ref[pl.ds(k * 2, 2), :, :, cols].reshape(256, 256) - dot3(
                get(l_s, lrow(k // 2, k % 2 * 256, 256), both), get(u_s, both, cols))

        for d in (0, 1):
            r = pl.ds(d * HALF, HALF)
            fc_ref[r, cols] = fc_ref[r, cols] - dot3(
                get(l_s, lrow(d, 768, HALF), both), get(u_s, both, cols))

        @pl.when(p == 0)
        def _():
            f_ref[0:NB, cols] = u0

            @pl.when((c == 0) & (i < 2))
            def _():
                f_ref[0:NB, cols] = t_ref[0:NB, cols]

        @pl.when(p == 1)
        def _():
            f_ref[0:NB, cols] = u1

            @pl.when((c == 1) & (i < 2))
            def _():
                f_ref[0:NB, cols] = t1

    def joined(r, k):
        return l_s[0, r, k].astype(F32) + l_s[1, r, k].astype(F32)

    for j in range(2):
        part = pl.ds(j * NB, NB)

        @pl.when(c == j)
        def _():
            f_ref[NB:, left] = joined(lrow(1, 0, NB), part)
            for d in (0, 1):
                fc_ref[pl.ds(d * HALF, HALF), left] = joined(lrow(d, 768, HALF), part)

            @pl.when(p > j)
            def _():
                f_ref[0:NB, left] = joined(lrow(0, 0, NB), part)

    @pl.when((c == 0) & (p == 1))
    def _():
        for d in (0, 1):
            f_ref[pl.ds(256 * d, 256), left] = joined(lrow(d, NB, 256), full)

    for g in (sa, oa, sb, ob):
        next(g)
    scatter_drain(0)
    scatter_drain(1)
    z_drain()


def factor(pack, take, csrc, matrix, li, ui):
    dma = pltpu.SemaphoreType.DMA
    return pl.pallas_call(
        factor_kernel,
        out_shape=(
            jax.ShapeDtypeStruct((1024, 1024), F32),
            jax.ShapeDtypeStruct((CAP, 1024), F32),
        ),
        in_specs=[spec(SM)] * 3 + [spec(VM)] * 3,
        out_specs=(spec(VM), spec(VM)),
        scratch_shapes=[
            VM((16, CAP, NB), F32),
            VM((16, 2 * CHUNK, NB), F32),
            VM((16, CAP, NB), F32),
            VM((16, 2 * CHUNK, NB), F32),
            VM((2, 2, ROWS, NB), F32),
            VM((1024, 1024), F32),
            VM((2, 1024, 1024), BF16),
            VM((2, 2 * ROWS, 1024), BF16),
            VM((2, NB, NB), BF16),
            VM((4, NB, NB), BF16),
            VM((4, NB, NB), BF16),
            VM((2, 4, CHUNK, 256), F32),
            VM((2, 2, 4, CHUNK, 256), F32),
            dma((12,)), dma((2,)), dma((4,)), dma((24,)), dma((8,)), dma((8,)),
            dma((160,)), dma((160,)),
            dma((STREAM,)), dma((STREAM,)), dma((STREAM,)), dma((STREAM,)),
            dma((2 * STREAM,)), dma((2 * STREAM,)),
        ],
        compiler_params=pltpu.CompilerParams(collective_id=0, has_side_effects=True,
                                             vmem_limit_bytes=67043328),
        name="factor",
    )(pack, take, csrc, matrix.reshape(8, 4, CHUNK, 1024), li, ui)


def place_kernel(cpos_ref, count_ref, f_ref, fc_ref, o_ref):
    o_ref[...] = f_ref[...]

    def one(k, carry):
        o_ref[pl.ds(cpos_ref[k], 1), :] = fc_ref[pl.ds(k, 1), :]
        return carry

    lax.fori_loop(0, count_ref[0], one, 0)


def place(cpos, count, f, fc):
    return pl.pallas_call(
        place_kernel,
        out_shape=jax.ShapeDtypeStruct((1024, 1024), F32),
        in_specs=[spec(SM), spec(SM), spec(VM), spec(VM)],
        out_specs=spec(VM),
        name="place",
    )(cpos, count, f, fc)


def spread(value, axis, source):
    kept = jnp.where(lax.axis_index(axis) == source, value, 0).astype(value.dtype)
    return lax.psum(kept, axis)


def duplicate_kernel(a_ref, o_ref):
    o_ref[...] = a_ref[...]


def duplicate(matrix):
    return pl.pallas_call(
        duplicate_kernel, out_shape=jax.ShapeDtypeStruct(matrix.shape, F32),
        in_specs=[spec(VM)], out_specs=spec(VM), name="duplicate",
    )(matrix)


def general(matrix, pivots, lower_inverses, upper_inverses):
    my_row = lax.axis_index("prow")
    my_col = lax.axis_index("pcol")
    rows_local, cols_local = matrix.shape
    dot = functools.partial(jnp.dot, precision=lax.Precision.HIGH, preferred_element_type=F32)
    row_blocks = jnp.arange(rows_local, dtype=jnp.int32) // NB * 16 + my_row
    col_blocks = jnp.arange(cols_local, dtype=jnp.int32) // NB * 16 + my_col

    def panel(step, current):
        targets = pivots[step]
        blocks = targets // NB
        slot = blocks // 16 * NB + targets % NB
        is_mine = blocks % 16 == my_row
        picked = jnp.where(is_mine[:, None], current[slot], 0.0)
        old_top = spread(current[:NB], "prow", step)
        new_top = lax.psum(picked, "prow")
        after = (col_blocks > step)[None, :]
        top = jnp.where(after, dot(lower_inverses[step], new_top), new_top)
        current = current.at[jnp.where(is_mine, slot, rows_local)].set(old_top, mode="drop")
        current = current.at[:NB].set(jnp.where(my_row == step, top, current[:NB]))
        column = spread(current[:, :NB], "pcol", step)
        below = (row_blocks > step)[:, None]
        lower = jnp.where(below, dot(column, upper_inverses[step]), 0.0)
        current = current - dot(lower, jnp.where(after, top, 0.0))
        return current.at[:, :NB].set(
            jnp.where(below & (my_col == step), lower, current[:, :NB]))

    return lax.fori_loop(0, 2, panel, duplicate(matrix))


def body(matrix, pivots, lower_inverses, upper_inverses):
    pack, take, csrc, cpos, total, fits = tables(pivots, lax.axis_index("prow"))

    def fast():
        return place(cpos, total, *factor(pack, take, csrc, matrix,
                                          lower_inverses, upper_inverses))

    return lax.cond(
        fits, fast, lambda: general(matrix, pivots, lower_inverses, upper_inverses))


def solution(mesh):
    placed = (P("prow", "pcol"), P(), P(), P())
    return jax.shard_map(
        body, mesh=mesh, in_specs=placed, out_specs=P("prow", "pcol"), check_vma=False
    )
```

time: 606 us -> 181 us (0.30)
  waiting for transfers between devices: 458 us -> 0 us
  Pallas kernels: 0 us -> 158 us
  local copies, waits for them, and re-layouts: 60.3 us -> 0.87 us
  matrix products: 44.6 us -> 0 us
  other arithmetic: 25.6 us -> 6.77 us
    psum x4 -> x0, waiting for transfers between devices: 458 us -> none  [spread(): return lax.psum(kept, axis)]
    pallas_call x0 -> x2, Pallas kernels: none -> 158 us  [the longest x1 152 us: factor(): pl.pallas_call(factor_kernel, out_shape=(jax.ShapeDtypeStruct((1024, 1024...]
    dot_general x6 -> x0, matrix products: 44.6 us -> none  [the longest x2 17.5 us: body(): jnp.dot(lower_part, upper_part, precision=lax.Precision.HIGHEST, preferre...]
    scatter x6 -> x0, local copies, waits for them, and re-layouts: 34.1 us -> none  [the longest x4 23.4 us: body(): current = current.at[dropped_slot].set(old_top, mode='drop')]
    select_n x9 -> x2, other arithmetic: 17 us -> 0.7 us  [held(): return jnp.where(hit > 0, hit - 1, default)]
    gather x4 -> x0, local copies, waits for them, and re-layouts: 15.7 us -> none  [body(): picked = jnp.where(is_mine[:, None], current[local_slot], 0.0)]
    scatter x2 -> x0, other arithmetic: 7.84 us -> none  [body(): current.at[:, :panel_width]]
    unnamed x8 -> x4, local copies, waits for them, and re-layouts: 6.65 us -> 0.01 us
  transfers between devices with their start and end apart: 4 -> 0, of which waited for: 4 -> 0; matrix products, arithmetic and copies ran while one was open for 0% -> 0% of each run, Pallas kernels for 0% -> 0%
where the time goes in v2:
time: 181 us; the launch traced here: 180 us
  Pallas kernels  158 us (87%)
  between operations  14.2 us (8%)
  other arithmetic  6.77 us (4%)
    pallas_call x1, Pallas kernels, factor(): pl.pallas_call(factor_kernel, out_shape=(jax.ShapeDtypeStruct((1024, 1024...  152 us
    pallas_call x1, Pallas kernels, place(): pl.pallas_call(place_kernel, out_shape=jax.ShapeDtypeStruct((1024, 1024),...  5.63 us

profile of v2, /device:TPU:35, one launch (start us, length us, event | category | flops | bytes accessed | tf_op | source)
XLA Modules:
  0.0 179.7 jit_solution(1568305571400183312)
XLA Ops:
  6.5 0.8 fusion.48
  7.3 0.4 select_reduce_fusion.5
  7.8 0.7 reshape_select_fusion
  8.5 0.0 copy-start.3
  8.5 0.0 copy-start.4
  8.5 0.5 convert_reduce_fusion.1
  9.0 0.6 reduce_max.46
  10.3 0.0 copy-done.3
  10.3 0.0 copy-done.4
  10.3 0.7 select_reduce_fusion.3
  11.0 0.2 convert_reduce_fusion
  11.3 0.1 fusion.39
  11.5 161.4 %conditional.1 = (f32[1024,1024]{1,0:T(8,128)}) conditional(s32[]{:T(128)} %convert_element_type.23, (f32[1024,1024]{1,0:T(8,128)}, s32[2,512]{1,0:T(2,128)}, f32[2,512,512]{2,1,0:T(8,128)}, f32[2,512,512]{2,1,0:T(8,128)}) %tuple.52, (f32[1024,1024]{1,0:T(8,128)}, s32[1024]{0:T(1024)}, s32[1024]{0:T(1024)}, pred[96,1024]{1,0:T(8,128)(4,1)S(1)}, ...), branch_computations={%region_11.19_spmd, %region_19.20_spmd} | conditional | flops 6450381824 | bytes 130078240 | solution.py:683
  11.7 1.3 fusion.7
  13.0 0.7 eq.217
  13.7 0.8 select_reduce_fusion.1
  14.5 0.7 reduce_sum.63
  15.2 152.0 %factor.1 = (f32[1024,1024]{1,0:T(8,128)}, f32[96,1024]{1,0:T(8,128)}) custom-call(s32[96]{0:T(128)} %get-tuple-element.470.pack_ref, s32[1024]{0:T(1024)} %get-tuple-element.503.take_ref, s32[96]{0:T(128)} %get-tuple-element.469.csrc_ref, f32[8,4,32,1024]{3,2,1,0:T(8,128)} %bitcast.50, f32[2,512,512]{2,1,0:T(8,128)} %get-tuple-element.360.li_ref, ...), custom_call_target="tpu_custom_call" | custom-call | tf_op jit(solution)/shard_map/cond/branch_1_fun/factor/pallas_call | solution.py:577
  167.2 5.6 %place.1 = f32[1024,1024]{1,0:T(8,128)} custom-call(s32[96]{0:T(128)} %get-tuple-element.471.cpos_ref, s32[1]{0:T(128)} %bitcast.count_ref, f32[1024,1024]{1,0:T(8,128)} %get-tuple-element.362.f_ref, f32[96,1024]{1,0:T(8,128)} %get-tuple-element.363.fc_ref), custom_call_target="tpu_custom_call" | custom-call | tf_op jit(solution)/shard_map/cond/branch_1_fun/place/pallas_call | solution.py:621
  (13 shorter events, 0.1 us)
Async XLA Ops:
  8.5 1.8 %copy-start.3 = (s32[1024]{0:T(1024)}, s32[1024]{0:T(1024)S(1)}, u32[]{:S(2)}) copy-start(s32[1024]{0:T(1024)S(1)} %get-tuple-element.511) | copy-start | bytes 12292
  8.5 1.9 %copy-start.4 = (s32[1024]{0:T(1024)}, s32[1024]{0:T(1024)S(1)}, u32[]{:S(2)}) copy-start(s32[1024]{0:T(1024)S(1)} %get-tuple-element.514) | copy-start | bytes 12292

commit v3 on v2

--- a/solution.py
+++ b/solution.py
@@ -13,7 +13,7 @@
 HALF = CAP // 2
 ZROWS = 16
 ROWS = 768 + HALF
-STREAM = ROWS // ZROWS
+STREAM = 768 // ZROWS
 SKEW = 5
 VM = pltpu.VMEM
 SM = pltpu.SMEM
@@ -49,7 +49,6 @@
     k = jnp.arange(CAP, dtype=jnp.int32)
     mine = (owner == me)[None, :] & (rank[None, :] == k[:, None])
     pack = jnp.sum(jnp.where(mine, local[None, :], 0), axis=1)
-    take = owner * 256 + rank
     second = held(i + NB, i + NB)
     g = (((r >> 9) << 4) + me) * NB + (r & 511)
     m1 = jnp.max(jnp.where(g[:, None] == p1[None, :], second[None, :] + 1, 0), axis=1)
@@ -59,10 +58,10 @@
     count = jnp.sum((valid[None, :] & (r[None, :] < r[:, None])).astype(jnp.int32), axis=1)
     chosen = valid[None, :] & (count[None, :] == k[:, None])
     cpos = jnp.sum(jnp.where(chosen, r[None, :], 0), axis=1)
-    csrc = ((src & 511) >> 5) * 256 + (src >> 9) * CHUNK + (src & 31)
-    csrc = jnp.sum(jnp.where(chosen, csrc[None, :], 0), axis=1)
+    csrc = jnp.sum(jnp.where(chosen, src[None, :], 0), axis=1)
+    came = (csrc & 511) >> 5, (csrc >> 9) * CHUNK + (csrc & 31)
     total = jnp.sum(valid.astype(jnp.int32)).reshape(1)
-    return pack, take, csrc, cpos, total, jnp.max(rank) < CAP
+    return (pack, owner, rank) + came, cpos, total, jnp.max(rank) < CAP
 
 
 def split(v):
@@ -85,11 +84,12 @@
     return ref[0, rows, cols], ref[1, rows, cols]
 
 
-def factor_kernel(pack_ref, take_ref, csrc_ref, a_ref, li_ref, ui_ref, f_ref, fc_ref,
+def factor_kernel(pack_ref, tq_ref, tr_ref, cq_ref, cr_ref, a_ref, li_ref, ui_ref, f_ref, fc_ref,
                   sa_ref, oa_ref, sb_ref, ob_ref, pp_ref, t_ref, u_s, l_s, uc_s, li_s, ui_s, sta, stb,
                   sc_send, sca_recv, scb_recv, sc2_send, sc2_recv, loc_sem,
                   ag_send, ag_recv,
-                  up_send, up_recv, dn_send, dn_recv, sib_send, sib_recv):
+                  up_send, up_recv, dn_send, dn_recv, sib_send, sib_recv,
+                  far_send, far_recv, pair_send, pair_recv):
     p = lax.axis_index("prow")
     x, y = p // 4, p % 4
     c = lax.axis_index("pcol")
@@ -109,8 +109,8 @@
     for d in (1, 2, 3):
         signal(barrier, at((x + d) % 4, y))
         signal(barrier, at(x, (y + d) % 4))
-    signal(barrier, zat((z + 1) % 8, core))
-    signal(barrier, zat((z + 7) % 8, core))
+    for d in range(1, 8):
+        signal(barrier, zat((z + d) % 8, core))
     signal(barrier, zat(z, 1 - core))
 
     def packed_row(k, carry):
@@ -129,11 +129,7 @@
             pp_ref[core, i // 16, pl.ds(pl.multiple_of(i % 16 * 32, 32), 32), :] = (
                 a_ref[i // 4, i % 4, :, 0:NB])
 
-    for j in range(2):
-        li_s[2 * j], li_s[2 * j + 1] = split(li_ref[j])
-        ui_s[2 * j], ui_s[2 * j + 1] = split(ui_ref[j])
-
-    pl.semaphore_wait(barrier, 9)
+    pl.semaphore_wait(barrier, 14)
 
     def quarter(i):
         return pl.ds(256 * i, 256)
@@ -373,8 +369,11 @@
             return carry
         lax.fori_loop(0, STREAM, sent, 0)
 
-    def landed(buffer, v):
-        return buffer[v // 256, pl.ds(v % 256, 1), :]
+    def top(buffer, r):
+        return buffer[tq_ref[r], pl.ds(tr_ref[r], 1), :]
+
+    def came(buffer, k):
+        return buffer[cq_ref[k], pl.ds(cr_ref[k], 1), :]
 
     left, right = pl.ds(0, NB), pl.ds(NB, NB)
 
@@ -382,8 +381,7 @@
         @pl.when(z == 0)
         def _():
             def one(r, carry):
-                v = take_ref[r + NB * (1 - core)]
-                pp_ref[core, r // 256, pl.ds(NB + r % 256, 1), :] = landed(sa_ref, v)
+                pp_ref[core, r // 256, pl.ds(NB + r % 256, 1), :] = top(sa_ref, r + NB * (1 - core))
                 return carry
             lax.fori_loop(0, NB, one, 0, unroll=8)
             z_source(32, 48)
@@ -392,56 +390,77 @@
         @pl.when(z == 0)
         def _():
             def one(k, carry):
-                pp_ref[core, k // HALF, pl.ds(768 + k % HALF, 1), :] = landed(oa_ref, csrc_ref[k])
+                pp_ref[core, k // HALF, pl.ds(768 + k % HALF, 1), :] = came(oa_ref, k)
                 return carry
             lax.fori_loop(0, CAP, one, 0, unroll=8)
-            z_source(48, STREAM)
+            for d in (4, 3, 5, 2, 6, 1, 7):
+                far(d).start()
+
+    def swapped_part(which):
+        return pp_ref.at[which, :, pl.ds(768, HALF), :]
+
+    def far(d):
+        ref = swapped_part(core)
+        return remote(ref, ref, far_send.at[d - 1], far_recv.at[0], zat(d, core))
+
+    def pair(which):
+        ref = swapped_part(which)
+        return remote(ref, ref, pair_send.at[0], pair_recv.at[0], zat(z, 1 - core))
+
+    def swapped_pair():
+        @pl.when(z != 0)
+        def _():
+            far(1).wait_recv()
+        pair(core).start()
 
     sa, oa = all_gather(0, 0), all_gather(0, 1)
     sb, ob = all_gather(1, 0), all_gather(1, 1)
     next(sa)
-    scatter(0)
-    scatter(1)
 
     @pl.when(z == 0)
     def _():
         z_source(0, 32)
 
-    z_relay(5, 8)
+    for j in range(2):
+        li_s[2 * j], li_s[2 * j + 1] = split(li_ref[j])
+        ui_s[2 * j], ui_s[2 * j + 1] = split(ui_ref[j])
+    z_relay(5, 9)
     next(sa)
-    z_relay(8, 13)
+    z_relay(9, 13)
     next(sa)
+    scatter(0)
+    z_relay(13, 23)
+    next(sa)
+    z_relay(23, 29)
+    next(sa)
+    panel_tops()
+    next(sb)
+    scatter(1)
+    z_relay(29, 33)
     relay(0)
-    z_relay(13, 20)
-    relay(1)
-    next(sb)
-    z_relay(20, 26)
-    next(sa)
+    z_relay(33, 42)
     scattered(0)
     next(oa)
-    z_relay(26, 32)
+    z_relay(42, 45)
+    next(sb)
+    z_relay(45, 50)
     next(oa)
-    z_relay(32, 36)
-    next(oa)
-    next(sa)
-    panel_tops()
-    z_relay(36, 44)
+    z_relay(50, 54)
     next(oa)
     next(sb)
-    z_relay(44, 50)
+    z_relay(54, 57)
+    relay(1)
+    z_relay(57, 62)
+    next(oa)
+    next(sb)
+    z_relay(62, 70)
     next(oa)
     panel_swapped()
+    z_relay(70, 76)
     next(sb)
     scattered(1)
     next(ob)
-    z_relay(50, 60)
-    next(sb)
-    next(ob)
-    z_relay(60, 68)
-    next(ob)
-    next(sb)
-    z_relay(68, STREAM + 7 * SKEW)
-    next(ob)
+    z_relay(76, STREAM + 7 * SKEW)
     z_finish()
 
     full = pl.ds(0, NB)
@@ -456,12 +475,12 @@
         return ref[2 * j, r, k], ref[2 * j + 1, r, k]
 
     def top_row(r, carry):
-        v = take_ref[r]
-        t_ref[pl.ds(r, 1), left] = landed(sa_ref, v)
-        t_ref[pl.ds(r, 1), right] = landed(sb_ref, v)
+        t_ref[pl.ds(r, 1), left] = top(sa_ref, r)
+        t_ref[pl.ds(r, 1), right] = top(sb_ref, r)
         return carry
 
     lax.fori_loop(0, 2 * NB, top_row, 0, unroll=8)
+    next(ob)
 
     def lower0(d, r, n):
         src = pl.ds(pl.multiple_of(r, 16), n)
@@ -472,36 +491,19 @@
         rest = pp_ref[1, d, src, :] - dot3(get(l_s, lrow(d, r, n), full), get(uc_s, full, full))
         put(l_s, lrow(d, r, n), pl.ds(NB, NB), dot3(split(rest), inv(ui_s, 1, full, full)))
 
-    @pl.loop(0, 2)
-    def _(i):
-        uc = sum(
-            dot3(inv(li_s, 0, full, tile(d)), split(pp_ref[1, d, pl.ds(NB, 256), tile(i)]))
-            for d in (0, 1)
-        )
-        put(uc_s, full, tile(i), uc)
-
-    @pl.loop(0, 6)
-    def _(i):
-        lower0(i // 3, i % 3 * 256, 256)
-
-    @pl.loop(0, 4)
-    def _(i):
-        lower1(i // 2, i % 2 * 256, 256)
+    put(uc_s, full, full, sum(
+        dot3(inv(li_s, 0, full, tile(d)), split(pp_ref[1, d, pl.ds(NB, 256), :]))
+        for d in (0, 1)
+    ))
+    next(ob)
 
     @pl.loop(0, 2)
     def _(d):
-        lower0(d, 768, HALF)
-        lower1(d, 768, HALF)
-
+        lower0(d, 0, 768)
+        lower1(d, 0, 512)
+
+    swapped_pair()
     next(ob)
-
-    def swapped_row(k, carry):
-        v = csrc_ref[k]
-        fc_ref[pl.ds(k, 1), left] = landed(oa_ref, v)
-        fc_ref[pl.ds(k, 1), right] = landed(ob_ref, v)
-        return carry
-
-    lax.fori_loop(0, CAP, swapped_row, 0, unroll=8)
     both = pl.ds(0, 2 * NB)
 
     @pl.loop(0, 4)
@@ -517,32 +519,50 @@
         u1 = dot3(inv(li_s, 1, full, full), split(t1))
         put(u_s, pl.ds(NB, NB), cols, u1)
 
-        @pl.loop(0, 4)
+        @pl.loop(0, 2)
         def _(k):
-            r = tile(k)
-            f_ref[r, cols] = a_ref[pl.ds(k * 2, 2), :, :, cols].reshape(256, 256) - dot3(
-                get(l_s, lrow(k // 2, k % 2 * 256, 256), both), get(u_s, both, cols))
-
+            r = tile(k, 512)
+            f_ref[r, cols] = a_ref[pl.ds(k * 4, 4), :, :, cols].reshape(512, 256) - dot3(
+                get(l_s, lrow(k, 0, 512), both), get(u_s, both, cols))
+
+        @pl.when(p == 0)
+        def _():
+            f_ref[0:NB, cols] = u0
+
+            @pl.when((c == 0) & (i < 2))
+            def _():
+                f_ref[0:NB, cols] = t_ref[0:NB, cols]
+
+        @pl.when(p == 1)
+        def _():
+            f_ref[0:NB, cols] = u1
+
+            @pl.when((c == 1) & (i < 2))
+            def _():
+                f_ref[0:NB, cols] = t1
+
+    next(ob)
+
+    def swapped_row(k, carry):
+        fc_ref[pl.ds(k, 1), left] = came(oa_ref, k)
+        fc_ref[pl.ds(k, 1), right] = came(ob_ref, k)
+        return carry
+
+    lax.fori_loop(0, CAP, swapped_row, 0, unroll=8)
+    pair(1 - core).wait_recv()
+
+    @pl.loop(0, 2)
+    def _(d):
+        lower0(d, 768, HALF)
+        lower1(d, 768, HALF)
+
+    @pl.loop(0, 4)
+    def _(i):
+        cols = tile(i)
         for d in (0, 1):
             r = pl.ds(d * HALF, HALF)
             fc_ref[r, cols] = fc_ref[r, cols] - dot3(
                 get(l_s, lrow(d, 768, HALF), both), get(u_s, both, cols))
-
-        @pl.when(p == 0)
-        def _():
-            f_ref[0:NB, cols] = u0
-
-            @pl.when((c == 0) & (i < 2))
-            def _():
-                f_ref[0:NB, cols] = t_ref[0:NB, cols]
-
-        @pl.when(p == 1)
-        def _():
-            f_ref[0:NB, cols] = u1
-
-            @pl.when((c == 1) & (i < 2))
-            def _():
-                f_ref[0:NB, cols] = t1
 
     def joined(r, k):
         return l_s[0, r, k].astype(F32) + l_s[1, r, k].astype(F32)
@@ -570,9 +590,15 @@
     scatter_drain(0)
     scatter_drain(1)
     z_drain()
-
-
-def factor(pack, take, csrc, matrix, li, ui):
+    pair(core).wait_send()
+
+    @pl.when(z == 0)
+    def _():
+        for d in range(1, 8):
+            far(d).wait_send()
+
+
+def factor(rows, matrix, li, ui):
     dma = pltpu.SemaphoreType.DMA
     return pl.pallas_call(
         factor_kernel,
@@ -580,7 +606,7 @@
             jax.ShapeDtypeStruct((1024, 1024), F32),
             jax.ShapeDtypeStruct((CAP, 1024), F32),
         ),
-        in_specs=[spec(SM)] * 3 + [spec(VM)] * 3,
+        in_specs=[spec(SM)] * 5 + [spec(VM)] * 3,
         out_specs=(spec(VM), spec(VM)),
         scratch_shapes=[
             VM((16, CAP, NB), F32),
@@ -600,11 +626,12 @@
             dma((160,)), dma((160,)),
             dma((STREAM,)), dma((STREAM,)), dma((STREAM,)), dma((STREAM,)),
             dma((2 * STREAM,)), dma((2 * STREAM,)),
+            dma((7,)), dma((1,)), dma((1,)), dma((1,)),
         ],
         compiler_params=pltpu.CompilerParams(collective_id=0, has_side_effects=True,
                                              vmem_limit_bytes=67043328),
         name="factor",
-    )(pack, take, csrc, matrix.reshape(8, 4, CHUNK, 1024), li, ui)
+    )(*rows, matrix.reshape(8, 4, CHUNK, 1024), li, ui)
 
 
 def place_kernel(cpos_ref, count_ref, f_ref, fc_ref, o_ref):
@@ -627,9 +654,19 @@
     )(cpos, count, f, fc)
 
 
+def ring_sum(value, axis):
+    ring = [(i, (i + 1) % 16) for i in range(16)]
+
+    def step(_, carry):
+        total, moving = carry
+        moving = lax.ppermute(moving, axis, ring)
+        return total + moving, moving
+
+    return lax.fori_loop(0, 15, step, (value, value))[0]
+
+
 def spread(value, axis, source):
-    kept = jnp.where(lax.axis_index(axis) == source, value, 0).astype(value.dtype)
-    return lax.psum(kept, axis)
+    return ring_sum(jnp.where(lax.axis_index(axis) == source, value, 0.0), axis)
 
 
 def duplicate_kernel(a_ref, o_ref):
@@ -658,7 +695,7 @@
         is_mine = blocks % 16 == my_row
         picked = jnp.where(is_mine[:, None], current[slot], 0.0)
         old_top = spread(current[:NB], "prow", step)
-        new_top = lax.psum(picked, "prow")
+        new_top = ring_sum(picked, "prow")
         after = (col_blocks > step)[None, :]
         top = jnp.where(after, dot(lower_inverses[step], new_top), new_top)
         current = current.at[jnp.where(is_mine, slot, rows_local)].set(old_top, mode="drop")
@@ -674,11 +711,10 @@
 
 
 def body(matrix, pivots, lower_inverses, upper_inverses):
-    pack, take, csrc, cpos, total, fits = tables(pivots, lax.axis_index("prow"))
+    rows, cpos, total, fits = tables(pivots, lax.axis_index("prow"))
 
     def fast():
-        return place(cpos, total, *factor(pack, take, csrc, matrix,
-                                          lower_inverses, upper_inverses))
+        return place(cpos, total, *factor(rows, matrix, lower_inverses, upper_inverses))
 
     return lax.cond(
         fits, fast, lambda: general(matrix, pivots, lower_inverses, upper_inverses))

time: 181 us -> 146 us (0.81)
  Pallas kernels: 158 us -> 136 us
  between operations: 14.2 us -> 0.74 us
    pallas_call x1, Pallas kernels: 152 us -> 131 us  [factor(): pl.pallas_call(factor_kernel, out_shape=(jax.ShapeDtypeStruct((1024, 1024...]
where the time goes in v3:
time: 146 us
  Pallas kernels  136 us (93%)
  other arithmetic  6.78 us (5%)
    pallas_call x1, Pallas kernels, factor(): pl.pallas_call(factor_kernel, out_shape=(jax.ShapeDtypeStruct((1024, 1024...  131 us
    pallas_call x1, Pallas kernels, place(): pl.pallas_call(place_kernel, out_shape=jax.ShapeDtypeStruct((1024, 1024),...  5.45 us

profile of v3, /device:TPU:35, one launch (start us, length us, event | category | flops | bytes accessed | tf_op | source)
XLA Modules:
  0.0 145.6 jit_solution(4840438660800912909)
XLA Ops:
  0.0 0.8 fusion.46
  0.8 0.4 select_reduce_fusion.4
  1.2 0.7 select_reduce_fusion.2
  1.9 0.6 fusion.44
  2.5 0.2 convert_reduce_fusion
  2.8 0.1 fusion.37
  2.8 0.2 select_reduce_fusion.6
  3.0 0.7 reshape_select_fusion
  3.7 0.5 convert_reduce_fusion.1
  4.4 0.6 reduce_max.46
  5.7 140.0 %conditional.1 = (f32[1024,1024]{1,0:T(8,128)}) conditional(s32[]{:T(128)} %convert_element_type.13, (f32[1024,1024]{1,0:T(8,128)}, s32[2,512]{1,0:T(2,128)}, f32[2,512,512]{2,1,0:T(8,128)}, f32[2,512,512]{2,1,0:T(8,128)}) %tuple.64, (f32[1024,1024]{1,0:T(8,128)}, s32[1024]{0:T(1024)S(1)}, s32[1024]{0:T(1024)S(1)}, s32[1024]{0:T(1024)S(1)}, ...), branch_computations={%region_11.22_spmd, %region_22.23_spmd} | conditional | flops 6450383872 | bytes 220257952 | solution.py:719
  5.9 0.0 copy-start.13
  5.9 0.0 copy-start.12
  5.9 0.6 copy-done.13
  6.5 0.8 select_reduce_fusion.1
  7.3 0.0 copy-done.12
  7.3 0.6 fusion.5
  7.9 130.9 %factor.1 = (f32[1024,1024]{1,0:T(8,128)}, f32[96,1024]{1,0:T(8,128)}) custom-call(s32[96]{0:T(128)} %get-tuple-element.517.pack_ref, s32[1024]{0:T(1024)} %copy-done.13, s32[1024]{0:T(1024)} %copy-done.12, s32[96]{0:T(128)} %get-tuple-element.565.cq_ref, s32[96]{0:T(128)} %get-tuple-element.564.cr_ref, f32[8,4,32,1024]{3,2,1,0:T(8,128)} %bitcast.50, ...), custom_call_target="tpu_custom_call" | custom-call | tf_op jit(solution)/shard_map/cond/branch_1_fun/factor/pallas_call | solution.py:603
  138.9 1.3 reduce_sum.62
  140.2 5.5 %place.1 = f32[1024,1024]{1,0:T(8,128)} custom-call(s32[96]{0:T(128)} %get-tuple-element.518.cpos_ref, s32[1]{0:T(128)} %bitcast.count_ref, f32[1024,1024]{1,0:T(8,128)} %get-tuple-element.416.f_ref, f32[96,1024]{1,0:T(8,128)} %get-tuple-element.417.fc_ref), custom_call_target="tpu_custom_call" | custom-call | tf_op jit(solution)/shard_map/cond/branch_1_fun/place/pallas_call | solution.py:648
  (13 shorter events, 0.1 us)
Async XLA Ops:
  5.9 0.6 copy-start.13
  5.9 1.4 copy-start.12

commit v4 on v3

--- a/solution.py
+++ b/solution.py
@@ -456,23 +456,43 @@
     z_relay(62, 70)
     next(oa)
     panel_swapped()
-    z_relay(70, 76)
+    z_relay(70, STREAM + 7 * SKEW)
+    z_finish()
+
+    full = pl.ds(0, NB)
+
+    def tile(i, size=256):
+        return pl.ds(pl.multiple_of(i * size, size), size)
+
+    def lrow(d, r, n):
+        return pl.ds(pl.multiple_of(d * ROWS + r, 16), n)
+
+    def inv(ref, j, r, k):
+        return ref[2 * j, r, k], ref[2 * j + 1, r, k]
+
+    def lower0(d, r, n):
+        src = pl.ds(pl.multiple_of(r, 16), n)
+        put(l_s, lrow(d, r, n), full, dot3(split(pp_ref[0, d, src, :]), inv(ui_s, 0, full, full)))
+
+    def lower1(d, r, n):
+        src = pl.ds(pl.multiple_of(r, 16), n)
+        rest = pp_ref[1, d, src, :] - dot3(get(l_s, lrow(d, r, n), full), get(uc_s, full, full))
+        put(l_s, lrow(d, r, n), pl.ds(NB, NB), dot3(split(rest), inv(ui_s, 1, full, full)))
+
+    put(uc_s, full, full, sum(
+        dot3(inv(li_s, 0, full, tile(d)), split(pp_ref[1, d, pl.ds(NB, 256), :]))
+        for d in (0, 1)
+    ))
     next(sb)
     scattered(1)
     next(ob)
-    z_relay(76, STREAM + 7 * SKEW)
-    z_finish()
-
-    full = pl.ds(0, NB)
-
-    def tile(i, size=256):
-        return pl.ds(pl.multiple_of(i * size, size), size)
-
-    def lrow(d, r, n):
-        return pl.ds(pl.multiple_of(d * ROWS + r, 16), n)
-
-    def inv(ref, j, r, k):
-        return ref[2 * j, r, k], ref[2 * j + 1, r, k]
+    lower0(0, 0, 768)
+    lower1(0, 0, 512)
+    next(ob)
+    lower0(1, 0, 768)
+    lower1(1, 0, 512)
+    next(ob)
+    swapped_pair()
 
     def top_row(r, carry):
         t_ref[pl.ds(r, 1), left] = top(sa_ref, r)
@@ -480,29 +500,6 @@
         return carry
 
     lax.fori_loop(0, 2 * NB, top_row, 0, unroll=8)
-    next(ob)
-
-    def lower0(d, r, n):
-        src = pl.ds(pl.multiple_of(r, 16), n)
-        put(l_s, lrow(d, r, n), full, dot3(split(pp_ref[0, d, src, :]), inv(ui_s, 0, full, full)))
-
-    def lower1(d, r, n):
-        src = pl.ds(pl.multiple_of(r, 16), n)
-        rest = pp_ref[1, d, src, :] - dot3(get(l_s, lrow(d, r, n), full), get(uc_s, full, full))
-        put(l_s, lrow(d, r, n), pl.ds(NB, NB), dot3(split(rest), inv(ui_s, 1, full, full)))
-
-    put(uc_s, full, full, sum(
-        dot3(inv(li_s, 0, full, tile(d)), split(pp_ref[1, d, pl.ds(NB, 256), :]))
-        for d in (0, 1)
-    ))
-    next(ob)
-
-    @pl.loop(0, 2)
-    def _(d):
-        lower0(d, 0, 768)
-        lower1(d, 0, 512)
-
-    swapped_pair()
     next(ob)
     both = pl.ds(0, 2 * NB)
 

time: 146 us -> 145 us (level)
  no operation moved by 1% of the time
where the time goes in v4:
time: 145 us
  Pallas kernels  136 us (94%)
  other arithmetic  6.78 us (5%)
    pallas_call x1, Pallas kernels, factor(): pl.pallas_call(factor_kernel, out_shape=(jax.ShapeDtypeStruct((1024, 1024...  130 us
    pallas_call x1, Pallas kernels, place(): pl.pallas_call(place_kernel, out_shape=jax.ShapeDtypeStruct((1024, 1024),...  5.57 us

profile of v4, /device:TPU:35, one launch (start us, length us, event | category | flops | bytes accessed | tf_op | source)
XLA Modules:
  0.0 144.8 jit_solution(4190513940665117850)
XLA Ops:
  0.0 0.8 fusion.46
  0.8 0.4 select_reduce_fusion.4
  1.2 0.7 select_reduce_fusion.2
  1.9 0.6 fusion.44
  2.5 0.2 convert_reduce_fusion
  2.8 0.1 fusion.37
  2.8 0.2 select_reduce_fusion.6
  3.0 0.7 reshape_select_fusion
  3.7 0.5 convert_reduce_fusion.1
  4.4 0.6 reduce_max.46
  5.7 139.1 %conditional.1 = (f32[1024,1024]{1,0:T(8,128)}) conditional(s32[]{:T(128)} %convert_element_type.13, (f32[1024,1024]{1,0:T(8,128)}, s32[2,512]{1,0:T(2,128)}, f32[2,512,512]{2,1,0:T(8,128)}, f32[2,512,512]{2,1,0:T(8,128)}) %tuple.64, (f32[1024,1024]{1,0:T(8,128)}, s32[1024]{0:T(1024)S(1)}, s32[1024]{0:T(1024)S(1)}, s32[1024]{0:T(1024)S(1)}, ...), branch_computations={%region_11.22_spmd, %region_22.23_spmd} | conditional | flops 6450383872 | bytes 220257952 | solution.py:716
  5.9 0.0 copy-start.13
  5.9 0.0 copy-start.12
  5.9 0.6 copy-done.13
  6.5 0.8 select_reduce_fusion.1
  7.3 0.0 copy-done.12
  7.3 0.6 fusion.5
  7.9 130.0 %factor.1 = (f32[1024,1024]{1,0:T(8,128)}, f32[96,1024]{1,0:T(8,128)}) custom-call(s32[96]{0:T(128)} %get-tuple-element.517.pack_ref, s32[1024]{0:T(1024)} %copy-done.13, s32[1024]{0:T(1024)} %copy-done.12, s32[96]{0:T(128)} %get-tuple-element.565.cq_ref, s32[96]{0:T(128)} %get-tuple-element.564.cr_ref, f32[8,4,32,1024]{3,2,1,0:T(8,128)} %bitcast.50, ...), custom_call_target="tpu_custom_call" | custom-call | tf_op jit(solution)/shard_map/cond/branch_1_fun/factor/pallas_call | solution.py:600
  137.9 1.3 reduce_sum.62
  139.2 5.6 %place.1 = f32[1024,1024]{1,0:T(8,128)} custom-call(s32[96]{0:T(128)} %get-tuple-element.518.cpos_ref, s32[1]{0:T(128)} %bitcast.count_ref, f32[1024,1024]{1,0:T(8,128)} %get-tuple-element.416.f_ref, f32[96,1024]{1,0:T(8,128)} %get-tuple-element.417.fc_ref), custom_call_target="tpu_custom_call" | custom-call | tf_op jit(solution)/shard_map/cond/branch_1_fun/place/pallas_call | solution.py:645
  (13 shorter events, 0.1 us)
Async XLA Ops:
  5.9 0.6 copy-start.13
  5.9 1.4 copy-start.12
